TPU v7x, 16 devices: a whole 2x2x2 slice. The times are simulated.
16 devices in a mesh: dp: 4 (over z, y), tp: 4 (over x, core).
Axes of the slice: x: 2, y: 2, z: 2, core: 2. Of those that a mesh axis runs over, the one named last changes fastest.
Arguments:
- token_ids: int32 [4, 1024], P('dp'), parts along dimension 0
- emb_table: bfloat16 [32000, 2048], P('tp')
- norm_gain: bfloat16 [2048], replicated
- grad_out: bfloat16 [4, 1024, 2048], P('dp', 'tp'), parts along dimension 0
Outputs:
- output 1: bfloat16 [4, 1024, 2048], P('dp', 'tp'), parts along dimension 0
- output 2: float32 [128000, 2048], P(('dp', 'tp')), parts along dimension 0
- output 3: float32 [8192], P('dp'), parts along dimension 0
There are 4 independent parts. A program takes and returns all parts, laid end to end along the dimension named above; an argument that names none is the same for every part.
All inputs are finite; a program needn't handle non-finite values.
Results may differ from a plain program's by a relative error of at most 0.00852867.
Values are sent between devices in bfloat16 or wider.
A program may use at most 1 GiB of HBM per device.

v0:
```python
import jax
import jax.numpy as jnp
from jax import lax
from jax.sharding import PartitionSpec as P

RMS_EPS = 1e-5


def norm_pass(embedded, norm_gain, grad_block):
    hidden_f32 = embedded.astype(jnp.float32)
    inv_rms = lax.rsqrt(jnp.mean(hidden_f32 * hidden_f32, axis=-1, keepdims=True) + RMS_EPS)
    x_hat = hidden_f32 * inv_rms
    normed = x_hat.astype(jnp.bfloat16) * norm_gain
    grad_f32 = grad_block.astype(jnp.float32)
    gain_part = jnp.sum(grad_f32 * x_hat, axis=(0, 1))
    grad_hat = grad_f32 * norm_gain.astype(jnp.float32)
    grad_in = (inv_rms * (grad_hat - x_hat * jnp.mean(grad_hat * x_hat, axis=-1, keepdims=True))).astype(jnp.bfloat16)
    return normed, grad_in, gain_part


def device_step(token_ids, table_block, norm_gain, grad_block):
    rows_block, hidden_size = table_block.shape
    tp_index = lax.axis_index('tp')
    local_ids = token_ids - tp_index * rows_block
    owned = (local_ids >= 0) & (local_ids < rows_block)
    looked_up = jnp.take(table_block, jnp.where(owned, local_ids, 0), axis=0)
    partial_rows = jnp.where(owned[:, :, None], looked_up, jnp.zeros((), jnp.bfloat16))
    embedded = lax.psum_scatter(partial_rows, 'tp', scatter_dimension=1, tiled=True)
    normed, grad_in, gain_part = norm_pass(embedded, norm_gain, grad_block)
    grad_gain = lax.psum(gain_part, 'tp')
    grad_all = lax.all_gather(grad_in, 'tp', axis=1, tiled=True)
    segment_ids = jnp.where(owned, local_ids, rows_block).reshape(-1)
    grad_table = jax.ops.segment_sum(grad_all.astype(jnp.float32).reshape(-1, hidden_size), segment_ids, num_segments=rows_block)
    return normed, grad_table, grad_gain


def solution(mesh):
    return jax.shard_map(device_step, mesh=mesh, in_specs=(P('dp', None), P('tp', None), P(None), P('dp', 'tp', None)), out_specs=(P('dp', 'tp', None), P(('dp', 'tp'), None), P('dp')), check_vma=False)
```

profile of v0, /device:TPU:0, one launch (start us, length us, event | category | flops | bytes accessed | tf_op | source)
XLA Modules:
  0.0 216.2 jit_solution(7055879801954122778)
XLA Ops:
  7.2 0.0 reduce-scatter.2.cloned.1.call-start
  7.2 0.7 and_reduce_fusion
  8.0 46.0 %gather_fusion = bf16[1024,2048]{1,0:T(8,128)(2,1)} fusion(bf16[8000,2048]{1,0:T(8,128)(2,1)} %param.5, s32[1024]{0:T(1024)S(1)} %broadcast_clamp_fusion.1), kind=kCustom, calls=%fused_computation | custom fusion | bytes 8392704 | tf_op jit(solution)/shard_map/jit(_take)/gather | solution.py:26
  53.9 4.1 %fusion.6 = bf16[1,1024,2048]{2,1,0:T(8,128)(2,1)} fusion(bf16[1024,2048]{1,0:T(8,128)(2,1)} %gather_fusion, pred[1024]{0:T(1024)(128)(4,1)S(1)} %get-tuple-element.7, pred[1024]{0:T(1024)(128)(4,1)S(1)} %get-tuple-element.9), kind=kLoop, calls=%fused_computation.8 | loop fusion | flops 4194304 | bytes 8390656 | tf_op jit(solution)/shard_map/jit(_where)/select_n | solution.py:27
  58.0 0.0 copy-start.2
  58.0 0.0 copy-start.1
  58.0 0.0 reduce-scatter.2.cloned.1.call-update
  58.0 0.0 copy-start.3
  58.0 0.0 all-gather.2.cloned.1.call-start
  58.1 0.6 copy-done.2
  58.7 44.4 %reduce-scatter.2.cloned.1.call-done = bf16[1,256,2048]{2,1,0:T(8,128)(2,1)} async-done(((bf16[1,1024,2048]{2,1,0:T(8,128)(2,1)}), bf16[1,256,2048]{2,1,0:T(8,128)(2,1)}) %reduce-scatter.2.cloned.1.call-update) | async-done | bytes 1048592 | tf_op jit(solution)/shard_map/reduce_scatter | solution.py:28
  103.1 1.6 fusion.14
  104.7 0.0 copy-done.1
  104.7 2.1 fusion.15
  106.8 2.8 %fusion.12 = bf16[1,256,2048]{2,1,0:T(8,128)(2,1)} fusion(bf16[1,256,2048]{2,1,0:T(8,128)(2,1)S(1)} %copy-done.1, bf16[1,256,2048]{2,1,0:T(8,128)(2,1)} %reduce-scatter.2.cloned.1.call-done, f32[256]{0:T(256)S(1)} %broadcast_multiply_fusion, f32[2048]{0:T(1024)S(1)} %convert_element_type.19, f32[256]{0:T(256)S(1)} %add_rsqrt_fusion), kind=kLoop, calls=%fused_computation.18 | loop fusion | flops 4194304 | bytes 3155968 | tf_op jit(solution)/shard_map/convert_element_type | solution.py:17
  109.5 0.0 all-gather.2.cloned.1.call-update
  109.5 0.0 copy-done.3
  109.6 3.8 %sort = (s32[1024]{0:T(1024)S(1)}, s32[1024]{0:T(1024)S(1)}) sort(s32[1024]{0:T(1024)S(1)} %bitcast.9, s32[1024]{0:T(1024)S(1)} %iota), dimensions={0}, to_apply=%compare | sort | flops 10240 | bytes 16384 | tf_op jit(solution)/shard_map/scatter-add | solution.py:33
  113.4 6.6 %psum.7 = f32[2048]{0:T(1024)} all-reduce(f32[2048]{0:T(1024)S(1)} %get-tuple-element.5), channel_id=1, replica_groups=mesh['dp'=4,'tp'=4] {'tp'}, use_global_device_ids=true, to_apply=%region_5.6 | all-reduce | flops 2048 | bytes 16384 | tf_op jit(solution)/shard_map/psum | solution.py:30
  120.0 0.0 copy-done
  120.0 1.3 fusion.16
  121.3 21.2 %all-gather.2.cloned.1.call-done = bf16[1,1024,2048]{2,1,0:T(8,128)(2,1)} async-done(((bf16[1,256,2048]{2,1,0:T(8,128)(2,1)}), bf16[1,1024,2048]{2,1,0:T(8,128)(2,1)}) %all-gather.2.cloned.1.call-update) | async-done | bytes 4194320 | tf_op jit(solution)/shard_map/all_gather | solution.py:31
  142.5 6.5 %bitcast_convert_fusion = f32[1024,2048]{1,0:T(8,128)} fusion(bf16[1,1024,2048]{2,1,0:T(8,128)(2,1)} %all-gather.2.cloned.1.call-done), kind=kLoop, calls=%fused_computation.6 | loop fusion | flops 2097152 | bytes 12582912 | tf_op jit(solution)/shard_map/reshape | solution.py:33
  148.9 60.4 %scatter_custom_fusion = f32[8000,2048]{1,0:T(8,128)} fusion(s32[1024]{0:T(1024)S(1)} %get-tuple-element.3, f32[]{:T(128)} %constant.15.clone.1, f32[1024,2048]{1,0:T(8,128)} %bitcast_convert_fusion, s32[1024]{0:T(1024)S(1)} %broadcast_clamp_fusion), kind=kCustom, calls=%fused_computation.3 | custom fusion | flops 2097152 | bytes 65536512 | tf_op jit(solution)/shard_map/scatter-add | solution.py:33
  (8 shorter events, 0.0 us)
Async XLA Ops:
  7.2 95.9 %reduce-scatter.2.cloned.1.call-start = ((), (), s32[]{:S(2)}) async-start(), calls=%async_computation.1 | async-start | bytes 5242880 | tf_op jit(solution)/shard_map/reduce_scatter | solution.py:28
  58.0 0.7 copy-start.2
  58.0 46.7 %copy-start.1 = (bf16[1,256,2048]{2,1,0:T(8,128)(2,1)S(1)}, bf16[1,256,2048]{2,1,0:T(8,128)(2,1)}, u32[]{:S(2)}) copy-start(bf16[1,256,2048]{2,1,0:T(8,128)(2,1)} %param.7) | copy-start | bytes 3145732
  58.0 51.5 %copy-start.3 = (s32[1,1024]{1,0:T(1,128)S(1)}, s32[1,1024]{1,0:T(1,128)}, u32[]{:S(2)}) copy-start(s32[1,1024]{1,0:T(1,128)} %param.4) | copy-start | bytes 12292
  58.0 84.4 %all-gather.2.cloned.1.call-start = ((), (), s32[]{:S(2)}) async-start(), calls=%async_computation.2 | async-start | bytes 5242880 | tf_op jit(solution)/shard_map/all_gather | solution.py:31
  103.1 16.9 %copy-start = (bf16[1,256,2048]{2,1,0:T(8,128)(2,1)S(1)}, bf16[1,256,2048]{2,1,0:T(8,128)(2,1)}, u32[]{:S(2)}) copy-start(bf16[1,256,2048]{2,1,0:T(8,128)(2,1)} %reduce-scatter.2.cloned.1.call-done) | copy-start | bytes 3145732
Sparse Core Ops, SparseCore 0:
  58.2 44.8 reduce-scatter.1
  109.7 32.7 all-gather.1
where the time goes:
time: 218 us; the launch traced here: 216 us
  other arithmetic  83.2 us (38%)
  waiting for transfers between devices  65.6 us (30%)
  local copies, waits for them, and re-layouts  46.6 us (21%)
  between operations  14.1 us (6%)
  blocking collectives  6.62 us (3%)
    scatter-add x3, other arithmetic, device_step(): jax.ops.segment_sum(grad_all.astype(jnp.float32).reshape(-1, hidden_size)...  64.2 us
    gather x1, local copies, waits for them, and re-layouts, device_step(): looked_up = jnp.take(table_block, jnp.where(owned, local_ids, 0), axis=0)  46 us
    reduce_scatter x1, waiting for transfers between devices, device_step(): lax.psum_scatter(partial_rows, 'tp', scatter_dimension=1, tiled=True)  44.4 us
    all_gather x1, waiting for transfers between devices, device_step(): grad_all = lax.all_gather(grad_in, 'tp', axis=1, tiled=True)  21.2 us
    psum x1, blocking collectives, device_step(): grad_gain = lax.psum(gain_part, 'tp')  6.62 us
    reshape x1, other arithmetic, device_step(): grad_all.astype(jnp.float32).reshape(-1, hidden_size)  6.48 us
  transfers between devices with their start and end apart: 2, of which 2 were waited for; matrix products, arithmetic and copies ran while one was open for 2% of the time, Pallas kernels for 0%

commit v1 on v0

v1 whole, which is shorter than its diff:
```python
import functools

import jax
import jax.numpy as jnp
from jax import lax
from jax.experimental import pallas as pl
from jax.experimental.pallas import tpu as pltpu
from jax.sharding import PartitionSpec as P

RMS_EPS = 1e-5
DY_CAP = 176
X_CAP = 96
U_CAP = 144
DY_SLOT = 192
SLAB = 8
KEY_STEP = 8192.0
NO_KEY = 1.0e6
ACROSS = [(i, i ^ 2) for i in range(4)]
SIBLING = [(i, i ^ 1) for i in range(4)]
F32 = jnp.float32
BF16 = jnp.bfloat16
ANY = pl.BlockSpec(memory_space=pl.ANY)
VMEM = pl.BlockSpec(memory_space=pltpu.VMEM)
SMEM = pl.BlockSpec(memory_space=pltpu.SMEM)


def dot(a, b, ca, cb):
    return lax.dot_general(a, b, (((ca,), (cb,)), ((), ())), preferred_element_type=F32)


def cost(us, moved):
    return pl.CostEstimate(flops=int(us * 2_000_000), bytes_accessed=moved, transcendentals=0)


def iota(shape, axis):
    return lax.broadcasted_iota(jnp.int32, shape, axis)


def owner_of(ids, rows):
    out = jnp.zeros_like(ids)
    for k in (1, 2, 3):
        out += jnp.where(ids >= k * rows, 1, 0)
    return out


def columns(row):
    parts = []
    for j in range(0, row.shape[1], 128):
        parts.append(jnp.broadcast_to(row[:, j:j + 128], (128, 128)).T)
    return jnp.concatenate(parts, axis=0)


def before(n):
    return jnp.where(iota((n, n), 0) < iota((n, n), 1), 1.0, 0.0).astype(BF16)


def pack_kernel(rows, ids_ref, dy_ref, out_ref):
    me = lax.axis_index('tp')
    span = dy_ref.shape[0]
    ids = ids_ref[:, pl.ds(pl.multiple_of(me * span, 128), span)]
    leaves = (owner_of(ids, rows) >= 2) != (me >= 2)
    flag = jnp.broadcast_to(jnp.where(leaves, 1.0, 0.0), (8, span))
    rank = dot(flag.astype(BF16), before(span), 1, 0)[0:1]
    rank = jnp.where(leaves, rank, -1.0)
    slots = iota((DY_CAP, span), 0).astype(F32)
    pick = jnp.where(slots == rank, 1.0, 0.0).astype(BF16)
    out_ref[...] = dot(pick, dy_ref[...], 1, 0).astype(BF16)


def index_kernel(rows, span, ids_ref, idx_ref, lst_ref, flag_ref, rank_ref, src_ref):
    me = lax.axis_index('tp')
    ids = ids_ref[...]
    n = ids.shape[1]
    owner = owner_of(ids, rows)
    local = ids - owner * rows
    pos = iota((1, n), 1)
    idf = ids.astype(F32)
    col = columns(idf)
    posc = iota((n, 128), 0).astype(F32)
    lo, hi = [], []
    for j in range(0, n, 128):
        same = col == idf[:, j:j + 128]
        lo.append(jnp.min(jnp.where(same, posc, 4096.0), axis=0, keepdims=True))
        hi.append(jnp.max(jnp.where(same, posc, -1.0), axis=0, keepdims=True))
    lo = jnp.concatenate(lo, axis=1)
    hi = jnp.concatenate(hi, axis=1)
    first = lo == pos.astype(F32)
    half = n // 2
    wanted = jnp.where(owner < 2, jnp.where(hi >= half, 1.0, 0.0), jnp.where(lo < half, 1.0, 0.0))
    key = (owner.astype(F32) * 2.0 + 1.0 - wanted) * KEY_STEP + local.astype(F32)
    keyf = jnp.where(first, key, NO_KEY)
    kcol = columns(keyf)
    rank = []
    for j in range(0, n, 128):
        rank.append(jnp.sum(jnp.where(kcol < key[:, j:j + 128], 1.0, 0.0), axis=0, keepdims=True))
    rank = jnp.concatenate(rank, axis=1)

    def below(bound):
        return jnp.sum(jnp.where(keyf < bound, 1.0, 0.0), axis=1, keepdims=True)

    base = [below(2.0 * KEY_STEP * o) for o in range(5)]
    over = jnp.zeros((1, 1), F32)
    for o in range(4):
        over = jnp.maximum(over, jnp.where(base[o + 1] - base[o] > U_CAP, 1.0, 0.0))
        over = jnp.maximum(over, jnp.where(below((2.0 * o + 1.0) * KEY_STEP) - base[o] > X_CAP, 1.0, 0.0))
    start = jnp.where(owner == 0, base[0], jnp.where(owner == 1, base[1], jnp.where(owner == 2, base[2], base[3])))
    uidx = rank - start
    mine = owner == me
    uidx_mine = jnp.where(mine, uidx, -1.0)
    idx_ref[0:1, :] = uidx_mine.astype(jnp.int32)

    crosses = (owner >= 2) != (pos >= half)
    flag = jnp.where(crosses, 1.0, 0.0)
    flags = jnp.concatenate([flag[:, h * span:(h + 1) * span] for h in range(4)] + [jnp.zeros((4, span), F32)], axis=0)
    ranks = dot(flags.astype(BF16), before(span), 1, 0)
    over = jnp.maximum(over, jnp.max(jnp.where(jnp.sum(flags, axis=1, keepdims=True) > DY_CAP, 1.0, 0.0), axis=0, keepdims=True))
    rank_ref[...] = jnp.where(flags > 0.5, ranks, -1.0)
    src_ref[0:1, :] = uidx_mine
    rel = owner ^ me
    offset = jnp.where(rel == 0, 0, jnp.where(rel == 1, U_CAP, jnp.where(rel == 2, 2 * U_CAP, 2 * U_CAP + X_CAP)))
    src_ref[1:2, :] = uidx + offset.astype(F32)
    slots = iota((span, span), 0).astype(F32)
    for row, flip in ((2, 2), (3, 3)):
        h = me ^ flip
        there = pl.ds(pl.multiple_of(h * span, 128), span)
        pick = jnp.where(slots == rank_ref[pl.ds(h, 1), :], 1.0, 0.0).astype(BF16)
        value = jnp.broadcast_to(src_ref[0:1, there] + 1.0, (8, span)).astype(BF16)
        idx_ref[row:row + 1, 0:span] = (dot(value, pick, 1, 1)[0:1] - 1.0).astype(jnp.int32)
    idx_ref[1:2, 0:span] = src_ref[1:2, pl.ds(pl.multiple_of(me * span, 128), span)].astype(jnp.int32)

    width = lst_ref.shape[1]
    lead_col = jnp.where(first & mine, uidx, -1.0)
    pick = jnp.where(iota((width, n), 0).astype(F32) == lead_col, 1.0, 0.0).astype(BF16)
    hi8 = local >> 8
    lo8 = local - hi8 * 256
    parts = jnp.concatenate([hi8.astype(F32), lo8.astype(F32), jnp.ones((1, n), F32), jnp.zeros((5, n), F32)], axis=0)
    got = dot(parts.astype(BF16), pick, 1, 1)
    row_of = got[0:1] * 256.0 + got[1:2]
    valid = got[2:3] > 0.5
    slab = jnp.where(valid, jnp.floor(row_of * (1.0 / SLAB)), -1.0)
    scol = columns(slab)
    slotc = iota((width, 128), 0).astype(F32)
    lead = []
    for j in range(0, width, 128):
        lead.append(jnp.min(jnp.where(scol == slab[:, j:j + 128], slotc, 4096.0), axis=0, keepdims=True))
    lead = jnp.concatenate(lead, axis=1)
    lst_ref[0:1, :] = row_of.astype(jnp.int32)
    lst_ref[1:2, :] = lead.astype(jnp.int32)
    count = jnp.sum(jnp.where(valid, 1.0, 0.0), axis=1, keepdims=True)
    lst_ref[2:3, :] = jnp.broadcast_to(jnp.minimum(count, float(U_CAP)), (1, width)).astype(jnp.int32)
    flag_ref[...] = jnp.broadcast_to(over, flag_ref.shape)


def gather_kernel(lst_ref, lrow_ref, table_ref, out_ref, slabs, sem):
    def issue(u, carry):
        pltpu.make_async_copy(table_ref.at[lst_ref[0, u] >> 3], slabs.at[u], sem).start()
        return carry

    lax.fori_loop(0, U_CAP, issue, 0, unroll=8)
    pltpu.make_async_copy(table_ref.at[pl.ds(0, U_CAP)], slabs, sem).wait()
    sub = lrow_ref[0:1, 0:U_CAP] & 7
    want = iota((1, U_CAP), 1) * SLAB + sub
    pick = jnp.where(iota((U_CAP * SLAB, U_CAP), 0) == want, 1.0, 0.0).astype(BF16)
    flat = slabs[...].reshape(U_CAP * SLAB, slabs.shape[2])
    out_ref[...] = dot(pick, flat, 0, 0).astype(BF16)


def dx_kernel(idx_ref, own_ref, sib_ref, got_ref, fwd_ref, u_ref, gain_ref, sum_ref, dg_ref, dy_all, pick_all, sems):
    me = lax.axis_index('tp')
    span = own_ref.shape[0]
    hidden = own_ref.shape[1]
    copies = []
    for k, (src, at) in enumerate(((own_ref, 0), (sib_ref, span), (got_ref, 2 * span), (fwd_ref, 2 * span + DY_SLOT))):
        copies.append(pltpu.make_async_copy(src, dy_all.at[pl.ds(at, src.shape[0])], sems.at[k]))
        copies[-1].start()
    for k in range(2):
        at = 2 * span + k * DY_SLOT
        dy_all[at + DY_CAP:at + DY_SLOT, :] = jnp.zeros((DY_SLOT - DY_CAP, hidden), BF16)
    own_row = idx_ref[0:1, pl.ds(pl.multiple_of(me * span, 128), span)]
    sib_row = idx_ref[0:1, pl.ds(pl.multiple_of((me ^ 1) * span, 128), span)]
    where_row = jnp.concatenate([own_row, sib_row, idx_ref[2:3, 0:DY_SLOT], idx_ref[3:4, 0:DY_SLOT]], axis=1)
    total = where_row.shape[1]
    pick_all[...] = jnp.where(iota((U_CAP, total), 0) == where_row, 1.0, 0.0).astype(BF16)
    sum_ref[...] = jnp.zeros_like(sum_ref)
    gain = gain_ref[...].astype(F32)
    ones = jnp.ones((U_CAP, 128), BF16)
    for c in copies:
        c.wait()

    def step(i, dg):
        at = pl.ds(pl.multiple_of(i * 128, 128), 128)
        pick = pick_all[:, at]
        h = dot(pick, u_ref[...], 0, 0)
        owned = dot(pick, ones, 0, 0)[:, 0:1] > 0.5
        r = lax.rsqrt(jnp.sum(h * h, axis=1, keepdims=True) * (1.0 / hidden) + RMS_EPS)
        xh = h * r
        dy = dy_all[at, :].astype(F32)
        u = dy * gain
        m = jnp.sum(u * xh, axis=1, keepdims=True) * (1.0 / hidden)
        dx = jnp.where(owned, r * (u - xh * m), 0.0).astype(BF16)
        sum_ref[...] += dot(pick, dx, 1, 0)
        return dg + jnp.sum((dy * xh).reshape(16, 8, hidden), axis=0)

    dg = lax.fori_loop(0, total // 128, step, jnp.zeros((8, hidden), F32))
    dg_ref[...] = jnp.sum(dg, axis=0, keepdims=True)


def slab_kernel(lst_ref, sum_ref, de_in, de_ref, stage, sem):
    del de_in
    count = lst_ref[2, 0]
    hidden = sum_ref.shape[1]
    sub = iota((SLAB, hidden), 0)

    def build(u, carry):
        lead = lst_ref[1, u]
        value = jnp.where(sub == (lst_ref[0, u] & 7), sum_ref[pl.ds(u, 1), :], 0.0)

        @pl.when(lead == u)
        def _():
            stage[u] = value

        @pl.when(lead != u)
        def _():
            stage[lead] += value

        return carry

    lax.fori_loop(0, count, build, 0)

    def send(u, carry):
        @pl.when(lst_ref[1, u] == u)
        def _():
            pltpu.make_async_copy(stage.at[u], de_ref.at[lst_ref[0, u] >> 3], sem).start()

        return carry

    lax.fori_loop(0, count, send, 0)

    def drain(u, carry):
        @pl.when(lst_ref[1, u] == u)
        def _():
            pltpu.make_async_copy(stage.at[u], de_ref.at[lst_ref[0, u] >> 3], sem).wait()

        return carry

    lax.fori_loop(0, count, drain, 0)


def zero_kernel(out_ref, zeros, sem):
    zeros[...] = jnp.zeros_like(zeros)
    step = zeros.shape[0]
    copies = [pltpu.make_async_copy(zeros, out_ref.at[pl.ds(i, step)], sem) for i in range(0, out_ref.shape[0], step)]
    for c in copies:
        c.start()
    for c in copies:
        c.wait()


def y_kernel(idx_ref, own_ref, sib_ref, got_ref, fwd_ref, gain_ref, g0, g1, g2, g3, y_ref, dg_ref, rows, sems):
    span, hidden = y_ref.shape
    copies = []
    at = 0
    for k, src in enumerate((own_ref, sib_ref, got_ref, fwd_ref)):
        copies.append(pltpu.make_async_copy(src, rows.at[pl.ds(at, src.shape[0])], sems.at[k]))
        copies[-1].start()
        at += src.shape[0]
    dg_ref[...] = (g0[...] + g1[...]) + (g2[...] + g3[...])
    pick = jnp.where(iota((rows.shape[0], span), 0) == idx_ref[1:2, 0:span], 1.0, 0.0).astype(BF16)
    for c in copies:
        c.wait()
    gain = gain_ref[...].astype(F32)
    for i in range(0, span, 128):
        h = dot(pick[:, i:i + 128], rows[...], 0, 0)
        r = lax.rsqrt(jnp.sum(h * h, axis=1, keepdims=True) * (1.0 / hidden) + RMS_EPS)
        y_ref[i:i + 128, :] = ((h * r).astype(BF16).astype(F32) * gain).astype(BF16)


def dense_step(token_ids, table_block, norm_gain, grad_block):
    rows_block, hidden = table_block.shape
    span = grad_block.shape[1]
    tp = lax.axis_index('tp')
    local_ids = token_ids[0] - tp * rows_block
    owned = (local_ids >= 0) & (local_ids < rows_block)
    looked_up = jnp.take(table_block, jnp.where(owned, local_ids, 0), axis=0)
    partial_rows = jnp.where(owned[:, None], looked_up, jnp.zeros((), BF16))
    embedded = lax.dynamic_slice(partial_rows, (tp * span, 0), (span, hidden))
    for flip in (1, 2, 3):
        block = lax.dynamic_slice(partial_rows, ((tp ^ flip) * span, 0), (span, hidden))
        embedded += lax.ppermute(block, 'tp', [(i, i ^ flip) for i in range(4)])
    h = embedded.astype(F32)
    r = lax.rsqrt(jnp.mean(h * h, axis=-1, keepdims=True) + RMS_EPS)
    xh = h * r
    y = xh.astype(BF16) * norm_gain
    dy = grad_block[0].astype(F32)
    dg = jnp.sum(dy * xh, axis=0)
    u = dy * norm_gain.astype(F32)
    dx = (r * (u - xh * jnp.mean(u * xh, axis=-1, keepdims=True))).astype(BF16)
    pair = dg + lax.ppermute(dg, 'tp', SIBLING)
    dg = pair + lax.ppermute(pair, 'tp', ACROSS)
    dx_all = jnp.zeros((4 * span, hidden), F32)
    for flip in (0, 1, 2, 3):
        block = dx if flip == 0 else lax.ppermute(dx, 'tp', [(i, i ^ flip) for i in range(4)])
        dx_all = lax.dynamic_update_slice(dx_all, block.astype(F32), ((tp ^ flip) * span, 0))
    segments = jnp.where(owned, local_ids, rows_block)
    de = jax.ops.segment_sum(dx_all, segments, num_segments=rows_block)
    return y, de, dg


def device_step(token_ids, table_block, norm_gain, grad_block):
    rows, hidden = table_block.shape
    n = token_ids.shape[1]
    span = grad_block.shape[1]
    dy = grad_block[0]
    gain = norm_gain.reshape(1, hidden)

    dy_sib = lax.ppermute(dy, 'tp', SIBLING)
    packed = pl.pallas_call(
        functools.partial(pack_kernel, rows), out_shape=jax.ShapeDtypeStruct((DY_CAP, hidden), BF16),
        in_specs=[VMEM, VMEM], out_specs=VMEM, cost_estimate=cost(2, 2 << 20), name='pack')(token_ids, dy)
    dy_got = lax.ppermute(packed, 'tp', ACROSS)
    idx, lst, over = pl.pallas_call(
        functools.partial(index_kernel, rows, span),
        out_shape=(jax.ShapeDtypeStruct((8, n), jnp.int32), jax.ShapeDtypeStruct((8, 256), jnp.int32),
                   jax.ShapeDtypeStruct((8, 128), F32)),
        in_specs=[VMEM], out_specs=(VMEM, VMEM, VMEM),
        scratch_shapes=[pltpu.VMEM((8, span), F32), pltpu.VMEM((8, n), F32)],
        cost_estimate=cost(3, 1 << 16), name='index')(token_ids)
    over = jnp.maximum(over, lax.ppermute(over, 'dp', [(i, i ^ 1) for i in range(4)]))
    over = jnp.maximum(over, lax.ppermute(over, 'dp', [(i, i ^ 2) for i in range(4)]))
    rows_u = pl.pallas_call(
        gather_kernel, out_shape=jax.ShapeDtypeStruct((U_CAP, hidden), BF16),
        in_specs=[SMEM, VMEM, ANY], out_specs=VMEM,
        scratch_shapes=[pltpu.VMEM((U_CAP, SLAB, hidden), BF16), pltpu.SemaphoreType.DMA],
        cost_estimate=cost(4, 6 << 20), name='gather')(lst, lst, table_block.reshape(rows // SLAB, SLAB, hidden))
    u_got = lax.ppermute(rows_u[:X_CAP], 'tp', ACROSS)
    u_sib = lax.ppermute(rows_u, 'tp', SIBLING)
    de = pl.pallas_call(
        zero_kernel, out_shape=jax.ShapeDtypeStruct((rows // SLAB, SLAB, hidden), F32),
        out_specs=ANY, scratch_shapes=[pltpu.VMEM((20, SLAB, hidden), F32), pltpu.SemaphoreType.DMA],
        cost_estimate=cost(20, 64 << 20), name='zero')()
    dy_fwd = lax.ppermute(dy_got, 'tp', SIBLING)
    sums, dg = pl.pallas_call(
        dx_kernel, out_shape=(jax.ShapeDtypeStruct((U_CAP, hidden), F32), jax.ShapeDtypeStruct((1, hidden), F32)),
        in_specs=[VMEM, ANY, ANY, ANY, ANY, VMEM, VMEM], out_specs=(VMEM, VMEM),
        scratch_shapes=[pltpu.VMEM((2 * span + 2 * DY_SLOT, hidden), BF16),
                        pltpu.VMEM((U_CAP, 2 * span + 2 * DY_SLOT), BF16), pltpu.SemaphoreType.DMA((4,))],
        cost_estimate=cost(7, 8 << 20), name='dx')(idx, dy, dy_sib, dy_got, dy_fwd, rows_u, gain)
    dgs = [dg] + [lax.ppermute(dg, 'tp', [(i, i ^ f) for i in range(4)]) for f in (1, 2, 3)]
    de = pl.pallas_call(
        slab_kernel, out_shape=jax.ShapeDtypeStruct((rows // SLAB, SLAB, hidden), F32),
        in_specs=[SMEM, VMEM, ANY], out_specs=ANY, input_output_aliases={2: 0},
        scratch_shapes=[pltpu.VMEM((U_CAP, SLAB, hidden), F32), pltpu.SemaphoreType.DMA],
        cost_estimate=cost(4, 8 << 20), name='slabs')(lst, sums, de)
    u_fwd = lax.ppermute(u_got, 'tp', SIBLING)
    y, dg = pl.pallas_call(
        y_kernel, out_shape=(jax.ShapeDtypeStruct((span, hidden), BF16), jax.ShapeDtypeStruct((1, hidden), F32)),
        in_specs=[VMEM, ANY, ANY, ANY, ANY, VMEM, VMEM, VMEM, VMEM, VMEM], out_specs=(VMEM, VMEM),
        scratch_shapes=[pltpu.VMEM((2 * U_CAP + 2 * X_CAP, hidden), BF16), pltpu.SemaphoreType.DMA((4,))],
        cost_estimate=cost(3, 4 << 20), name='y')(idx, rows_u, u_sib, u_got, u_fwd, gain, *dgs)

    def keep(y, de, dg):
        return y, de, dg

    def redo(y, de, dg):
        y, de, dg = dense_step(token_ids, table_block, norm_gain, grad_block)
        return y, de.reshape(rows // SLAB, SLAB, hidden), dg.reshape(1, hidden)

    y, de, dg = lax.cond(over[0, 0] > 0.5, redo, keep, y, de, dg)
    return y[None], de.reshape(rows, hidden), dg.reshape(hidden)


def solution(mesh):
    return jax.shard_map(device_step, mesh=mesh, in_specs=(P('dp', None), P('tp', None), P(None), P('dp', 'tp', None)), out_specs=(P('dp', 'tp', None), P(('dp', 'tp'), None), P('dp')), check_vma=False)
```

time: 218 us -> 86.6 us (0.40)
  other arithmetic: 83.2 us -> 0.01 us
  Pallas kernels: 0 us -> 54.6 us
  waiting for transfers between devices: 65.6 us -> 15.3 us
  local copies, waits for them, and re-layouts: 46.6 us -> 4.53 us
  between operations: 14.1 us -> 1.63 us
  starting transfers between devices: 0.08 us -> 9.28 us
  blocking collectives: 6.62 us -> 0 us
    scatter-add x3 -> x0, other arithmetic: 64.2 us -> none  [device_step(): jax.ops.segment_sum(grad_all.astype(jnp.float32).reshape(-1, hidden_size)...]
    pallas_call x0 -> x7, Pallas kernels: none -> 54.6 us  [the longest x1 20.6 us: device_step(): pl.pallas_call(zero_kernel, out_shape=jax.ShapeDtypeStruct((rows // SLAB,...]
    gather x1 -> x0, local copies, waits for them, and re-layouts: 46 us -> none  [device_step(): looked_up = jnp.take(table_block, jnp.where(owned, local_ids, 0), axis=0)]
    reduce_scatter x1 -> x0, waiting for transfers between devices: 44.4 us -> none  [device_step(): lax.psum_scatter(partial_rows, 'tp', scatter_dimension=1, tiled=True)]
    all_gather x1 -> x0, waiting for transfers between devices: 21.2 us -> none  [device_step(): grad_all = lax.all_gather(grad_in, 'tp', axis=1, tiled=True)]
    ppermute x0 -> x11, waiting for transfers between devices: none -> 15.3 us  [the longest x1 7.06 us: device_step(): u_got = lax.ppermute(rows_u[:X_CAP], 'tp', ACROSS)]
    ppermute x0 -> x11, starting transfers between devices: none -> 9.28 us  [the longest x1 3.23 us: device_step(): dy_got = lax.ppermute(packed, 'tp', ACROSS)]
    psum x1 -> x0, blocking collectives: 6.62 us -> none  [device_step(): grad_gain = lax.psum(gain_part, 'tp')]
  transfers between devices with their start and end apart: 2 -> 11, of which waited for: 2 -> 3; matrix products, arithmetic and copies ran while one was open for 2% -> 3% of each run, Pallas kernels for 0% -> 56%
where the time goes in v1:
time: 86.6 us; the launch traced here: 85.6 us
  Pallas kernels  54.6 us (63%)
  waiting for transfers between devices  15.3 us (18%)
  starting transfers between devices  9.28 us (11%)
  local copies, waits for them, and re-layouts  4.53 us (5%)
  between operations  1.63 us (2%)
    pallas_call x1, Pallas kernels, device_step(): pl.pallas_call(zero_kernel, out_shape=jax.ShapeDtypeStruct((rows // SLAB,...  20.6 us
    pallas_call x1, Pallas kernels, device_step(): pl.pallas_call(dx_kernel, out_shape=(jax.ShapeDtypeStruct((U_CAP, hidden)...  11.4 us
    ppermute x1, waiting for transfers between devices, device_step(): u_got = lax.ppermute(rows_u[:X_CAP], 'tp', ACROSS)  7.06 us
    ppermute x1, waiting for transfers between devices, device_step(): dy_got = lax.ppermute(packed, 'tp', ACROSS)  6.43 us
    pallas_call x1, Pallas kernels, device_step(): pl.pallas_call(gather_kernel, out_shape=jax.ShapeDtypeStruct((U_CAP, hidd...  6.37 us
    pallas_call x1, Pallas kernels, device_step(): pl.pallas_call(slab_kernel, out_shape=jax.ShapeDtypeStruct((rows // SLAB,...  6.11 us
    pallas_call x1, Pallas kernels, device_step(): pl.pallas_call(y_kernel, out_shape=(jax.ShapeDtypeStruct((span, hidden),...  4.37 us
    ppermute x1, starting transfers between devices, device_step(): dy_got = lax.ppermute(packed, 'tp', ACROSS)  3.23 us
  transfers between devices with their start and end apart: 11, of which 3 were waited for; matrix products, arithmetic and copies ran while one was open for 3% of the time, Pallas kernels for 56%

profile of v1, /device:TPU:0, one launch (start us, length us, event | category | flops | bytes accessed | tf_op | source)
XLA Modules:
  0.0 85.6 jit_solution(10631875810965503468)
XLA Ops:
  0.6 2.6 %pack.1 = bf16[176,2048]{1,0:T(8,128)(2,1)} custom-call(s32[1,1024]{1,0:T(1,128)} %ids_ref.3, bf16[256,2048]{1,0:T(8,128)(2,1)} %bitcast.22), custom_call_target="tpu_custom_call" | custom-call | flops 4000000 | bytes 2097152 | tf_op jit(solution)/shard_map/pack/pallas_call | solution.py:317
  3.2 3.2 %collective-permute-start.14 = (bf16[176,2048]{1,0:T(8,128)(2,1)}, bf16[176,2048]{1,0:T(8,128)(2,1)S(1)}, u32[]{:S(2)}, u32[]{:S(2)}) collective-permute-start(bf16[176,2048]{1,0:T(8,128)(2,1)} %pack.1), channel_id=1, source_target_pairs={{0,2},{1,3},{2,0},{3,1},{4,6},{5,7},{6,4},{7,5},{8,10},{9,11},{10,... | collective-permute-start | bytes 2162696 | tf_op jit(solution)/shard_map/ppermute | solution.py:320
  6.5 3.1 %index.1 = (s32[8,1024]{1,0:T(8,128)}, s32[8,256]{1,0:T(8,128)}, f32[8,128]{1,0:T(8,128)}) custom-call(s32[1,1024]{1,0:T(1,128)} %ids_ref.3), custom_call_target="tpu_custom_call" | custom-call | flops 6000000 | bytes 65536 | tf_op jit(solution)/shard_map/index/pallas_call | solution.py:321
  9.6 6.4 %gather.11.u_ref.own_ref = bf16[144,2048]{1,0:T(8,128)(2,1)} custom-call(s32[8,256]{1,0:T(8,128)} %get-tuple-element.39.lst_ref.lrow_ref, s32[8,256]{1,0:T(8,128)} %get-tuple-element.39.lst_ref.lrow_ref, bf16[1000,8,2048]{2,1,0:T(8,128)(2,1)} %bitcast.21), custom_call_target="tpu_custom_call" | custom-call | flops 8000000 | bytes 6291456 | tf_op jit(solution)/shard_map/gather/pallas_call | solution.py:330
  15.9 1.0 %slice.12 = bf16[96,2048]{1,0:T(8,128)(2,1)S(1)} slice(bf16[144,2048]{1,0:T(8,128)(2,1)} %gather.11.u_ref.own_ref), slice={[0:96], [0:2048]} | slice | bytes 786432 | tf_op jit(solution)/shard_map/slice | solution.py:335
  17.0 6.4 %collective-permute-done.14.got_ref = bf16[176,2048]{1,0:T(8,128)(2,1)S(1)} collective-permute-done((bf16[176,2048]{1,0:T(8,128)(2,1)}, bf16[176,2048]{1,0:T(8,128)(2,1)S(1)}, u32[]{:S(2)}, u32[]{:S(2)}) %collective-permute-start.14) | collective-permute-done | bytes 720928 | tf_op jit(solution)/shard_map/ppermute | solution.py:320
  23.5 0.5 collective-permute-start.10
  24.0 7.1 %collective-permute-done.11.got_ref = bf16[96,2048]{1,0:T(8,128)(2,1)} collective-permute-done((bf16[96,2048]{1,0:T(8,128)(2,1)S(1)}, bf16[96,2048]{1,0:T(8,128)(2,1)}, u32[]{:S(2)}, u32[]{:S(2)}) %collective-permute-start.11) | collective-permute-done | bytes 393248 | tf_op jit(solution)/shard_map/ppermute | solution.py:335
  31.0 1.8 %collective-permute-start.8 = (f32[8,128]{1,0:T(8,128)S(1)}, f32[8,128]{1,0:T(8,128)S(1)}, u32[]{:S(2)}, u32[]{:S(2)}) collective-permute-start(f32[8,128]{1,0:T(8,128)S(1)} %copy-done.12), channel_id=1, source_target_pairs={{0,4},{4,0},{8,12},{12,8},{1,5},{5,1},{9,13},{13,9},{2,6},{6,2},{1... | collective-permute-start | bytes 12296 | tf_op jit(solution)/shard_map/ppermute | solution.py:328
  32.8 1.8 %collective-permute-done.8 = f32[8,128]{1,0:T(8,128)S(1)} collective-permute-done((f32[8,128]{1,0:T(8,128)S(1)}, f32[8,128]{1,0:T(8,128)S(1)}, u32[]{:S(2)}, u32[]{:S(2)}) %collective-permute-start.8) | collective-permute-done | bytes 4128 | tf_op jit(solution)/shard_map/ppermute | solution.py:328
  34.6 1.8 %collective-permute-start.9 = (f32[8,128]{1,0:T(8,128)S(1)}, f32[8,128]{1,0:T(8,128)S(1)}, u32[]{:S(2)}, u32[]{:S(2)}) collective-permute-start(f32[8,128]{1,0:T(8,128)S(1)} %max.6), channel_id=1, source_target_pairs={{0,8},{4,12},{8,0},{12,4},{1,9},{5,13},{9,1},{13,5},{2,10},{6,14},... | collective-permute-start | bytes 12296 | tf_op jit(solution)/shard_map/ppermute | solution.py:329
  36.5 0.6 reshape.98.gain_ref
  37.1 0.9 %copy-done.3 = bf16[256,2048]{1,0:T(8,128)(2,1)} copy-done((bf16[256,2048]{1,0:T(8,128)(2,1)}, bf16[256,2048]{1,0:T(8,128)(2,1)S(1)}, u32[]{:S(2)}) %copy-start.3) | copy-done | bytes 1048600
  38.0 0.2 copy-done.6
  38.3 11.4 %dx.1 = (f32[144,2048]{1,0:T(8,128)}, f32[1,2048]{1,0:T(1,128)}) custom-call(s32[8,1024]{1,0:T(8,128)} %get-tuple-element.38.idx_ref, bf16[256,2048]{1,0:T(8,128)(2,1)S(1)} %bitcast.24, bf16[256,2048]{1,0:T(8,128)(2,1)} %copy-done.3, bf16[176,2048]{1,0:T(8,128)(2,1)} %copy-done.5, bf16[176,2048]{1,0:T(8,128)(2,1)} %copy-done.6, ...), custom_call_target="tpu_custom_call" | custom-call | flops 14000000 | bytes 8388608 | tf_op jit(solution)/shard_map/dx/pallas_call | solution.py:342
  49.9 1.4 %collective-permute-start.17 = (f32[1,2048]{1,0:T(1,128)}, f32[1,2048]{1,0:T(1,128)S(1)}, u32[]{:S(2)}, u32[]{:S(2)}) collective-permute-start(f32[1,2048]{1,0:T(1,128)} %get-tuple-element.40.g0), channel_id=1, source_target_pairs={{0,2},{1,3},{2,0},{3,1},{4,6},{5,7},{6,4},{7,5},{8,10},{9,11},{10,... | collective-permute-start | bytes 24584 | tf_op jit(solution)/shard_map/ppermute | solution.py:348
  51.3 0.3 collective-permute-start.16
  51.6 20.6 %zero.1.de_in = f32[1000,8,2048]{2,1,0:T(8,128)} custom-call(), custom_call_target="tpu_custom_call" | custom-call | flops 40000000 | bytes 67108864 | tf_op jit(solution)/shard_map/zero/pallas_call | solution.py:337
  72.2 0.5 slice.6
  73.4 6.1 %slabs.1 = f32[1000,8,2048]{2,1,0:T(8,128)} custom-call(s32[8,256]{1,0:T(8,128)} %get-tuple-element.39.lst_ref.lrow_ref, f32[144,2048]{1,0:T(8,128)} %get-tuple-element.42.sum_ref, f32[1000,8,2048]{2,1,0:T(8,128)} %zero.1.de_in), custom_call_target="tpu_custom_call", output_to_operand_aliasing={{}: (2, {})} | custom-call | flops 8000000 | bytes 8388608 | tf_op jit(solution)/shard_map/slabs/pallas_call | solution.py:349
  79.6 0.6 copy-done.9
  80.2 0.6 copy-done.11
  80.8 4.4 %y.1 = (bf16[256,2048]{1,0:T(8,128)(2,1)}, f32[1,2048]{1,0:T(1,128)}) custom-call(s32[8,1024]{1,0:T(8,128)} %get-tuple-element.38.idx_ref, bf16[144,2048]{1,0:T(8,128)(2,1)} %gather.11.u_ref.own_ref, bf16[144,2048]{1,0:T(8,128)(2,1)} %collective-permute-done.10.sib_ref, bf16[96,2048]{1,0:T(8,128)(2,1)} %collective-permute-done.11.got_ref, ...), custom_call_target="tpu_custom_call" | custom-call | flops 6000000 | bytes 4194304 | tf_op jit(solution)/shard_map/y/pallas_call | solution.py:355
  85.2 0.2 conditional.1
  (31 shorter events, 0.3 us)
Async XLA Ops:
  3.2 20.2 %collective-permute-start.14 = (bf16[176,2048]{1,0:T(8,128)(2,1)}, bf16[176,2048]{1,0:T(8,128)(2,1)S(1)}, u32[]{:S(2)}, u32[]{:S(2)}) collective-permute-start(bf16[176,2048]{1,0:T(8,128)(2,1)} %pack.1), channel_id=1, source_target_pairs={{0,2},{1,3},{2,0},{3,1},{4,6},{5,7},{6,4},{7,5},{8,10},{9,11},{10,... | collective-permute-start | bytes 2162696 | tf_op jit(solution)/shard_map/ppermute | solution.py:320
  6.5 30.6 %collective-permute-start.13 = (bf16[256,2048]{1,0:T(8,128)(2,1)}, bf16[256,2048]{1,0:T(8,128)(2,1)S(1)}, u32[]{:S(2)}, u32[]{:S(2)}) collective-permute-start(bf16[256,2048]{1,0:T(8,128)(2,1)} %bitcast.23), channel_id=1, source_target_pairs={{0,1},{1,0},{2,3},{3,2},{4,5},{5,4},{6,7},{7,6},{8,9},{9,8},{10,11... | collective-permute-start | bytes 3145736 | tf_op jit(solution)/shard_map/ppermute | solution.py:316
  9.6 21.5 %copy-start.12 = (f32[8,128]{1,0:T(8,128)S(1)}, f32[8,128]{1,0:T(8,128)}, u32[]{:S(2)}) copy-start(f32[8,128]{1,0:T(8,128)} %get-tuple-element.37) | copy-start | bytes 12292
  9.6 26.9 %copy-start.7 = (bf16[2048]{0:T(1024)(128)(2,1)S(1)}, bf16[2048]{0:T(1024)(128)(2,1)}, u32[]{:S(2)}) copy-start(bf16[2048]{0:T(1024)(128)(2,1)} %param.8) | copy-start | bytes 12292
  9.6 28.7 %copy-start = (bf16[1,256,2048]{2,1,0:T(8,128)(2,1)S(1)}, bf16[1,256,2048]{2,1,0:T(8,128)(2,1)}, u32[]{:S(2)}) copy-start(bf16[1,256,2048]{2,1,0:T(8,128)(2,1)} %param.9) | copy-start | bytes 3145732
  17.0 14.1 %collective-permute-start.11 = (bf16[96,2048]{1,0:T(8,128)(2,1)S(1)}, bf16[96,2048]{1,0:T(8,128)(2,1)}, u32[]{:S(2)}, u32[]{:S(2)}) collective-permute-start(bf16[96,2048]{1,0:T(8,128)(2,1)S(1)} %slice.12), channel_id=1, source_target_pairs={{0,2},{1,3},{2,0},{3,1},{4,6},{5,7},{6,4},{7,5},{8,10},{9,11},{10,... | collective-permute-start | bytes 1179656 | tf_op jit(solution)/shard_map/ppermute | solution.py:335
  23.4 13.6 %copy-start.5 = (bf16[176,2048]{1,0:T(8,128)(2,1)}, bf16[176,2048]{1,0:T(8,128)(2,1)S(1)}, u32[]{:S(2)}) copy-start(bf16[176,2048]{1,0:T(8,128)(2,1)S(1)} %collective-permute-done.14.got_ref) | copy-start | bytes 2162692
  23.5 13.6 %collective-permute-start.15 = (bf16[176,2048]{1,0:T(8,128)(2,1)S(1)}, bf16[176,2048]{1,0:T(8,128)(2,1)S(1)}, u32[]{:S(2)}, u32[]{:S(2)}) collective-permute-start(bf16[176,2048]{1,0:T(8,128)(2,1)S(1)} %collective-permute-done.14.got_ref), channel_id=1, source_target_pairs={{0,1},{1,0},{2,3},{3,2},{4,5},{5,4},{6,7},{7,6},{8,9},{9,8},{10,11... | collective-permute-start | bytes 2162696 | tf_op jit(solution)/shard_map/ppermute | solution.py:341
  23.5 56.1 %collective-permute-start.10 = (bf16[144,2048]{1,0:T(8,128)(2,1)}, bf16[144,2048]{1,0:T(8,128)(2,1)}, u32[]{:S(2)}, u32[]{:S(2)}) collective-permute-start(bf16[144,2048]{1,0:T(8,128)(2,1)} %gather.11.u_ref.own_ref), channel_id=1, source_target_pairs={{0,1},{1,0},{2,3},{3,2},{4,5},{5,4},{6,7},{7,6},{8,9},{9,8},{10,11... | collective-permute-start | bytes 1769480 | tf_op jit(solution)/shard_map/ppermute | solution.py:336
  31.0 48.5 %collective-permute-start.12 = (bf16[96,2048]{1,0:T(8,128)(2,1)}, bf16[96,2048]{1,0:T(8,128)(2,1)}, u32[]{:S(2)}, u32[]{:S(2)}) collective-permute-start(bf16[96,2048]{1,0:T(8,128)(2,1)} %collective-permute-done.11.got_ref), channel_id=1, source_target_pairs={{0,1},{1,0},{2,3},{3,2},{4,5},{5,4},{6,7},{7,6},{8,9},{9,8},{10,11... | collective-permute-start | bytes 1179656 | tf_op jit(solution)/shard_map/ppermute | solution.py:354
  31.0 3.6 %collective-permute-start.8 = (f32[8,128]{1,0:T(8,128)S(1)}, f32[8,128]{1,0:T(8,128)S(1)}, u32[]{:S(2)}, u32[]{:S(2)}) collective-permute-start(f32[8,128]{1,0:T(8,128)S(1)} %copy-done.12), channel_id=1, source_target_pairs={{0,4},{4,0},{8,12},{12,8},{1,5},{5,1},{9,13},{13,9},{2,6},{6,2},{1... | collective-permute-start | bytes 12296 | tf_op jit(solution)/shard_map/ppermute | solution.py:328
  34.6 16.7 %collective-permute-start.9 = (f32[8,128]{1,0:T(8,128)S(1)}, f32[8,128]{1,0:T(8,128)S(1)}, u32[]{:S(2)}, u32[]{:S(2)}) collective-permute-start(f32[8,128]{1,0:T(8,128)S(1)} %max.6), channel_id=1, source_target_pairs={{0,8},{4,12},{8,0},{12,4},{1,9},{5,13},{9,1},{13,5},{2,10},{6,14},... | collective-permute-start | bytes 12296 | tf_op jit(solution)/shard_map/ppermute | solution.py:329
  37.1 1.0 %copy-start.3 = (bf16[256,2048]{1,0:T(8,128)(2,1)}, bf16[256,2048]{1,0:T(8,128)(2,1)S(1)}, u32[]{:S(2)}) copy-start(bf16[256,2048]{1,0:T(8,128)(2,1)S(1)} %collective-permute-done.13.sib_ref) | copy-start | bytes 3145732
  37.1 1.2 %copy-start.6 = (bf16[176,2048]{1,0:T(8,128)(2,1)}, bf16[176,2048]{1,0:T(8,128)(2,1)S(1)}, u32[]{:S(2)}) copy-start(bf16[176,2048]{1,0:T(8,128)(2,1)S(1)} %collective-permute-done.15.fwd_ref) | copy-start | bytes 2162692
  49.7 29.8 %collective-permute-start.18 = (f32[1,2048]{1,0:T(1,128)}, f32[1,2048]{1,0:T(1,128)S(1)}, u32[]{:S(2)}, u32[]{:S(2)}) collective-permute-start(f32[1,2048]{1,0:T(1,128)} %get-tuple-element.40.g0), channel_id=1, source_target_pairs={{0,3},{1,2},{2,1},{3,0},{4,7},{5,6},{6,5},{7,4},{8,11},{9,10},{10,... | collective-permute-start | bytes 24584 | tf_op jit(solution)/shard_map/ppermute | solution.py:348
  49.9 29.6 %collective-permute-start.17 = (f32[1,2048]{1,0:T(1,128)}, f32[1,2048]{1,0:T(1,128)S(1)}, u32[]{:S(2)}, u32[]{:S(2)}) collective-permute-start(f32[1,2048]{1,0:T(1,128)} %get-tuple-element.40.g0), channel_id=1, source_target_pairs={{0,2},{1,3},{2,0},{3,1},{4,6},{5,7},{6,4},{7,5},{8,10},{9,11},{10,... | collective-permute-start | bytes 24584 | tf_op jit(solution)/shard_map/ppermute | solution.py:348
  51.3 28.3 %collective-permute-start.16 = (f32[1,2048]{1,0:T(1,128)}, f32[1,2048]{1,0:T(1,128)S(1)}, u32[]{:S(2)}, u32[]{:S(2)}) collective-permute-start(f32[1,2048]{1,0:T(1,128)} %get-tuple-element.40.g0), channel_id=1, source_target_pairs={{0,1},{1,0},{2,3},{3,2},{4,5},{5,4},{6,7},{7,6},{8,9},{9,8},{10,11... | collective-permute-start | bytes 24584 | tf_op jit(solution)/shard_map/ppermute | solution.py:348
  73.4 11.8 %copy-start.8 = (s32[1,1024]{1,0:T(1,128)S(1)}, s32[1,1024]{1,0:T(1,128)}, u32[]{:S(2)}) copy-start(s32[1,1024]{1,0:T(1,128)} %ids_ref.3) | copy-start | bytes 12292
  79.6 0.6 copy-start.9
  79.6 0.6 copy-start.10
  80.2 0.6 copy-start.11

commit v2 on v1

v2 whole, which is shorter than its diff:
```python
import functools

import jax
import jax.numpy as jnp
from jax import lax
from jax.experimental import pallas as pl
from jax.experimental.pallas import tpu as pltpu
from jax.sharding import PartitionSpec as P


RMS_EPS = 1e-5
DY_CAP = 176
X_CAP = 96
U_CAP = 144
GROUP = 16
FILL_STEP = 20
BUILD = 4
FILLS = (0, 300, 500, 600, 860, 940, 1000)
SLAB = 8
KEY_STEP = 8192.0
NO_KEY = 1.0e6
ACROSS = [(i, i ^ 2) for i in range(4)]
SIBLING = [(i, i ^ 1) for i in range(4)]
F32 = jnp.float32
BF16 = jnp.bfloat16
ANY = pl.BlockSpec(memory_space=pltpu.HBM)
VMEM = pl.BlockSpec(memory_space=pltpu.VMEM)
SMEM = pl.BlockSpec(memory_space=pltpu.SMEM)


def dot(a, b, ca, cb):
    return lax.dot_general(a, b, (((ca,), (cb,)), ((), ())), preferred_element_type=F32)


def cost(us, moved):
    return pl.CostEstimate(flops=int(us * 2_000_000), bytes_accessed=moved, transcendentals=0)


def iota(shape, axis):
    return lax.broadcasted_iota(jnp.int32, shape, axis)


def owner_of(ids, rows):
    out = jnp.zeros_like(ids)
    for k in (1, 2, 3):
        out += jnp.where(ids >= k * rows, 1, 0)
    return out


def columns(row):
    parts = []
    for j in range(0, row.shape[1], 128):
        parts.append(jnp.broadcast_to(row[:, j:j + 128], (128, 128)).T)
    return jnp.concatenate(parts, axis=0)


def before(n):
    return jnp.where(iota((n, n), 0) < iota((n, n), 1), 1.0, 0.0).astype(BF16)


def pack_kernel(rows, ids_ref, dy_ref, out_ref):
    me = lax.axis_index('tp')
    span = dy_ref.shape[0]
    ids = ids_ref[:, pl.ds(pl.multiple_of(me * span, 128), span)]
    leaves = (owner_of(ids, rows) >= 2) != (me >= 2)
    flag = jnp.broadcast_to(jnp.where(leaves, 1.0, 0.0), (8, span))
    rank = dot(flag.astype(BF16), before(span), 1, 0)[0:1]
    rank = jnp.where(leaves, rank, -1.0)
    slots = iota((DY_CAP, span), 0).astype(F32)
    pick = jnp.where(slots == rank, 1.0, 0.0).astype(BF16)
    out_ref[...] = dot(pick, dy_ref[...], 1, 0).astype(BF16)


def index_tables(rows, span, ids, rank_ref, src_ref, idx_ref, lst_ref, flag_ref):
    me = lax.axis_index('tp')
    n = ids.shape[1]
    owner = owner_of(ids, rows)
    local = ids - owner * rows
    pos = iota((1, n), 1)
    idf = ids.astype(F32)
    col = columns(idf)
    posc = iota((n, 128), 0).astype(F32)
    lo, hi = [], []
    for j in range(0, n, 128):
        same = col == idf[:, j:j + 128]
        lo.append(jnp.min(jnp.where(same, posc, 4096.0), axis=0, keepdims=True))
        hi.append(jnp.max(jnp.where(same, posc, -1.0), axis=0, keepdims=True))
    lo = jnp.concatenate(lo, axis=1)
    hi = jnp.concatenate(hi, axis=1)
    first = lo == pos.astype(F32)
    half = n // 2
    wanted = jnp.where(owner < 2, jnp.where(hi >= half, 1.0, 0.0), jnp.where(lo < half, 1.0, 0.0))
    key = (owner.astype(F32) * 2.0 + 1.0 - wanted) * KEY_STEP + local.astype(F32)
    keyf = jnp.where(first, key, NO_KEY)
    kcol = columns(keyf)
    rank = []
    for j in range(0, n, 128):
        rank.append(jnp.sum(jnp.where(kcol < key[:, j:j + 128], 1.0, 0.0), axis=0, keepdims=True))
    rank = jnp.concatenate(rank, axis=1)

    def below(bound):
        return jnp.sum(jnp.where(keyf < bound, 1.0, 0.0), axis=1, keepdims=True)

    base = [below(2.0 * KEY_STEP * o) for o in range(5)]
    over = jnp.zeros((1, 1), F32)
    for o in range(4):
        over = jnp.maximum(over, jnp.where(base[o + 1] - base[o] > U_CAP, 1.0, 0.0))
        over = jnp.maximum(over, jnp.where(below((2.0 * o + 1.0) * KEY_STEP) - base[o] > X_CAP, 1.0, 0.0))
    start = jnp.where(owner == 0, base[0], jnp.where(owner == 1, base[1], jnp.where(owner == 2, base[2], base[3])))
    uidx = rank - start
    mine = owner == me
    uidx_mine = jnp.where(mine, uidx, -1.0)

    crosses = (owner >= 2) != (pos >= half)
    flag = jnp.where(crosses, 1.0, 0.0)
    flags = jnp.concatenate([flag[:, h * span:(h + 1) * span] for h in range(4)] + [jnp.zeros((4, span), F32)], axis=0)
    ranks = dot(flags.astype(BF16), before(span), 1, 0)
    over = jnp.maximum(over, jnp.max(jnp.where(jnp.sum(flags, axis=1, keepdims=True) > DY_CAP, 1.0, 0.0), axis=0, keepdims=True))
    rank_ref[...] = jnp.where(flags > 0.5, ranks, -1.0)
    src_ref[0:1, :] = uidx_mine
    rel = owner ^ me
    offset = jnp.where(rel == 0, 0, jnp.where(rel == 1, U_CAP, jnp.where(rel == 2, 2 * U_CAP, 2 * U_CAP + X_CAP)))
    src_ref[1:2, :] = uidx + offset.astype(F32)
    slots = iota((span, span), 0).astype(F32)
    for row, flip in ((2, 2), (3, 3)):
        h = me ^ flip
        there = pl.ds(pl.multiple_of(h * span, 128), span)
        pick = jnp.where(slots == rank_ref[pl.ds(h, 1), :], 1.0, 0.0).astype(BF16)
        value = jnp.broadcast_to(src_ref[0:1, there] + 1.0, (8, span)).astype(BF16)
        idx_ref[row:row + 1, :] = (dot(value, pick, 1, 1)[0:1] - 1.0).astype(jnp.int32)
    for row, flip in ((0, 0), (1, 1)):
        there = pl.ds(pl.multiple_of((me ^ flip) * span, 128), span)
        idx_ref[row:row + 1, :] = src_ref[0:1, there].astype(jnp.int32)
    idx_ref[4:5, :] = src_ref[1:2, pl.ds(pl.multiple_of(me * span, 128), span)].astype(jnp.int32)

    width = lst_ref.shape[1]
    lead_col = jnp.where(first & mine, uidx, -1.0)
    pick = jnp.where(iota((width, n), 0).astype(F32) == lead_col, 1.0, 0.0).astype(BF16)
    hi8 = local >> 8
    lo8 = local - hi8 * 256
    parts = jnp.concatenate([hi8.astype(F32), lo8.astype(F32), jnp.ones((1, n), F32), jnp.zeros((5, n), F32)], axis=0)
    got = dot(parts.astype(BF16), pick, 1, 1)
    row_of = got[0:1] * 256.0 + got[1:2]
    valid = got[2:3] > 0.5
    slab = jnp.where(valid, jnp.floor(row_of * (1.0 / SLAB)), -1.0)
    scol = columns(slab)
    slotc = iota((width, 128), 0).astype(F32)
    lead = []
    for j in range(0, width, 128):
        same = scol == slab[:, j:j + 128]
        lead.append(jnp.min(jnp.where(same, slotc, 4096.0), axis=0, keepdims=True))
    lead = jnp.where(valid, jnp.concatenate(lead, axis=1), -1.0)
    slot = iota((1, width), 1).astype(F32)
    heads = jnp.where(lead == slot, 1.0, 0.0)
    others = jnp.where(valid & (lead != slot), 1.0, 0.0)
    kinds = jnp.concatenate([heads, others, jnp.zeros((6, width), F32)], axis=0)
    place = dot(kinds.astype(BF16), before(width), 1, 0)
    slots = iota((width, width), 0).astype(F32)
    hi8 = jnp.floor(slab * (1.0 / 256.0))
    values = jnp.concatenate([slot, lead, hi8, slab - hi8 * 256.0, jnp.zeros((4, width), F32)], axis=0).astype(BF16)
    pick = jnp.where(slots == jnp.where(heads > 0.5, place[0:1], -1.0), 1.0, 0.0).astype(BF16)
    head = dot(values, pick, 1, 1)
    pick = jnp.where(slots == jnp.where(others > 0.5, place[1:2], -1.0), 1.0, 0.0).astype(BF16)
    other = dot(values, pick, 1, 1)
    counts = jnp.sum(jnp.concatenate([jnp.where(valid, 1.0, 0.0), kinds[0:7]], axis=0), axis=1, keepdims=True)
    counts = jnp.minimum(jnp.broadcast_to(counts, (8, width)), float(U_CAP))
    lanes = iota((1, width), 1)
    lst_ref[0:1, :] = row_of.astype(jnp.int32)
    lst_ref[1:2, :] = jnp.minimum(head[0:1], U_CAP - 1.0).astype(jnp.int32)
    lst_ref[2:3, :] = (head[2:3] * 256.0 + head[3:4]).astype(jnp.int32)
    lst_ref[3:4, :] = jnp.minimum(other[0:1], U_CAP - 1.0).astype(jnp.int32)
    lst_ref[4:5, :] = jnp.minimum(other[1:2], U_CAP - 1.0).astype(jnp.int32)
    lst_ref[5:6, :] = jnp.where(lanes == 0, counts[0:1], jnp.where(lanes == 1, counts[1:2], counts[2:3])).astype(jnp.int32)
    flag_ref[...] = jnp.broadcast_to(over, flag_ref.shape)


class Fill:
    def __init__(self, de_ref, zeros, sem):
        self.de_ref, self.zeros, self.sem, self.copies = de_ref, zeros, sem, []

    def clear(self):
        self.zeros[...] = jnp.zeros_like(self.zeros)

    def start(self, lo, hi):
        step = self.zeros.shape[0]
        for at in range(lo, hi, step):
            n = min(step, hi - at)
            self.copies.append(pltpu.make_async_copy(self.zeros.at[pl.ds(0, n)], self.de_ref.at[pl.ds(at, n)], self.sem))
            self.copies[-1].start()

    def wait(self):
        for c in self.copies:
            c.wait()


def inverse_rms(u_ref):
    h = u_ref[...].astype(F32)
    r = lax.rsqrt(jnp.sum(h * h, axis=1, keepdims=True) * (1.0 / h.shape[1]) + RMS_EPS)
    a = r.astype(BF16).astype(F32)
    b = (r - a).astype(BF16).astype(F32)
    parts = [jnp.broadcast_to(p, (h.shape[0], 128)) for p in (a, b, r - a - b)]
    return jnp.concatenate(parts, axis=1).astype(BF16)


def token_block(where_row, u_ref, cols, dy_ref, gain_ref, h_ref, r_ref, m_ref, dx_ref, dg_ref):
    n, hidden = dy_ref.shape
    pick = jnp.where(iota((U_CAP, n), 0) == where_row, 1.0, 0.0).astype(BF16)
    h_ref[0:n, :] = dot(pick, u_ref[...], 0, 0)
    r = dot(pick, cols, 0, 0)
    r_ref[0:n, :] = r[:, 0:128] + r[:, 128:256] + r[:, 256:384]

    def first(i, carry):
        at = pl.ds(pl.multiple_of(i * GROUP, GROUP), GROUP)
        r = r_ref[at, :]
        acc = jnp.zeros((GROUP, 128), F32)
        for j in range(0, hidden, 128):
            xh = h_ref[at, j:j + 128] * r
            dy = dy_ref[at, j:j + 128].astype(F32)
            acc += (dy * gain_ref[:, j:j + 128]) * xh
            dg_ref[:, j:j + 128] += jnp.sum((dy * xh).reshape(GROUP // 8, 8, 128), axis=0)
        m_ref[at, :] = acc
        return carry

    lax.fori_loop(0, n // GROUP, first, 0)
    m_ref[0:n, :] = jnp.broadcast_to(jnp.sum(m_ref[0:n, :], axis=1, keepdims=True) * (1.0 / hidden), (n, 128))

    def second(i, carry):
        at = pl.ds(pl.multiple_of(i * GROUP, GROUP), GROUP)
        r, m = r_ref[at, :], m_ref[at, :]
        for j in range(0, hidden, 128):
            xh = h_ref[at, j:j + 128] * r
            u = dy_ref[at, j:j + 128].astype(F32) * gain_ref[:, j:j + 128]
            dx_ref[at, j:j + 128] = jnp.where(r > 0.0, r * (u - xh * m), 0.0).astype(BF16)
        return carry

    lax.fori_loop(0, n // GROUP, second, 0)
    return dot(pick, dx_ref[0:n, :], 1, 0)


def main_kernel(rows, ids_ref, own_ref, table_ref, gain_ref, idx_ref, lst_ref, flag_ref, u_ref, ux_ref, sum_ref,
                dg_ref, de_ref, rank_ref, src_ref, lst_smem, slabs, h_ref, r_ref, m_ref, dx_ref, g_ref, zeros, sems):
    hidden = own_ref.shape[1]
    fill = Fill(de_ref, zeros, sems.at[0])
    fill.clear()
    fill.start(FILLS[0], FILLS[1])
    index_tables(rows, own_ref.shape[0], ids_ref[...], rank_ref, src_ref, idx_ref, lst_ref, flag_ref)
    c = pltpu.make_async_copy(lst_ref, lst_smem, sems.at[1])
    c.start()
    c.wait()

    def issue(u, carry):
        pltpu.make_async_copy(table_ref.at[lst_smem[0, u] >> 3], slabs.at[u], sems.at[2]).start()
        return carry

    lax.fori_loop(0, U_CAP, issue, 0, unroll=8)
    want = iota((1, U_CAP), 1) * SLAB + (lst_ref[0:1, 0:U_CAP] & 7)
    pick = jnp.where(iota((U_CAP * SLAB, U_CAP), 0) == want, 1.0, 0.0).astype(BF16)
    dg_ref[...] = jnp.zeros_like(dg_ref)
    g_ref[...] = gain_ref[...].reshape(1, hidden).astype(F32)
    pltpu.make_async_copy(table_ref.at[pl.ds(0, U_CAP)], slabs, sems.at[2]).wait()
    fill.start(FILLS[1], FILLS[2])
    u_ref[...] = dot(pick, slabs[...].reshape(U_CAP * SLAB, hidden), 0, 0).astype(BF16)
    ux_ref[...] = u_ref[0:X_CAP, :]
    cols = inverse_rms(u_ref)
    sum_ref[...] = token_block(idx_ref[0:1, :], u_ref, cols, own_ref, g_ref, h_ref, r_ref, m_ref, dx_ref, dg_ref)
    fill.wait()


def zero_kernel(lo, hi, de_in, de_ref, zeros, sem):
    del de_in
    fill = Fill(de_ref, zeros, sem)
    fill.clear()
    fill.start(lo, hi)
    fill.wait()


def token_kernel(idx_ref, u_ref, us_ref, sib_ref, got_ref, fwd_ref, sumin_ref, dgin_ref, gain_ref, de_in,
                 sum_ref, dg_ref, part_ref, de_ref, h_ref, r_ref, m_ref, dx_ref, dg8_ref, g_ref, zeros, sem):
    del de_in
    hidden = u_ref.shape[1]
    fill = Fill(de_ref, zeros, sem)
    fill.clear()
    fill.start(FILLS[3], FILLS[4])
    cols = inverse_rms(u_ref)
    g_ref[...] = gain_ref[...].reshape(1, hidden).astype(F32)
    dg8_ref[...] = dgin_ref[...]
    sum_ref[...] = sumin_ref[...] + token_block(idx_ref[1:2, :], u_ref, cols, sib_ref, g_ref, h_ref, r_ref, m_ref, dx_ref, dg8_ref)
    sum_ref[...] += token_block(idx_ref[2:3, 0:DY_CAP], u_ref, cols, got_ref, g_ref, h_ref, r_ref, m_ref, dx_ref, dg8_ref)
    sum_ref[...] += token_block(idx_ref[3:4, 0:DY_CAP], u_ref, cols, fwd_ref, g_ref, h_ref, r_ref, m_ref, dx_ref, dg8_ref)
    dg_ref[...] = jnp.sum(dg8_ref[...], axis=0, keepdims=True)
    src = idx_ref[4:5, :]
    span = src.shape[1]
    part = jnp.zeros((span, hidden), F32)
    for k, ref in enumerate((u_ref, us_ref)):
        pick = jnp.where(iota((U_CAP, span), 0) + k * U_CAP == src, 1.0, 0.0).astype(BF16)
        part += dot(pick, ref[...], 0, 0)
    part_ref[...] = part.astype(BF16)
    fill.wait()


def final_kernel(tab_ref, flag_ref, idx_ref, sum_ref, part_ref, got_ref, fwd_ref, gain_ref, g0, g1, g2, g3, de_in,
                 y_ref, dg_ref, over_ref, de_ref, lst_ref, stage, h_ref, r_ref, g_ref, zeros, sems):
    del de_in
    span, hidden = y_ref.shape
    table = pltpu.make_async_copy(tab_ref, lst_ref, sems.at[2])
    table.start()
    fill = Fill(de_ref, zeros, sems.at[0])
    fill.clear()
    fill.start(FILLS[5], FILLS[6])
    over_ref[...] = flag_ref[0:1, 0:1].astype(jnp.int32)
    dg_ref[...] = (g0[...] + g1[...]) + (g2[...] + g3[...])
    g_ref[...] = gain_ref[...].reshape(1, hidden).astype(F32)
    sub = iota((SLAB, hidden), 0)
    src = idx_ref[4:5, :] - 2 * U_CAP
    for k, ref in enumerate((got_ref, fwd_ref)):
        pick = jnp.where(iota((X_CAP, span), 0) + k * X_CAP == src, 1.0, 0.0).astype(BF16)
        h = dot(pick, ref[...], 0, 0)
        h_ref[...] = h if k == 0 else h_ref[...] + h
    table.wait()
    count, heads, others = lst_ref[5, 0], lst_ref[5, 1], lst_ref[5, 2]

    def build(i, carry):
        for k in range(BUILD):
            u = i * BUILD + k
            stage[u] = jnp.where(sub == (lst_ref[0, u] & 7), sum_ref[pl.ds(u, 1), :], 0.0)
        return carry

    lax.fori_loop(0, (count + BUILD - 1) // BUILD, build, 0)

    def join(i, carry):
        stage[lst_ref[4, i]] += stage[lst_ref[3, i]]
        return carry

    lax.fori_loop(0, others, join, 0)
    fill.wait()

    def send(i):
        pltpu.make_async_copy(stage.at[lst_ref[1, i]], de_ref.at[lst_ref[2, i]], sems.at[1]).start()

    def send_some(i, carry):
        for k in range(BUILD):
            send(i * BUILD + k)
        return carry

    def send_one(i, carry):
        send(i)
        return carry

    lax.fori_loop(0, heads // BUILD, send_some, 0)
    lax.fori_loop(heads // BUILD * BUILD, heads, send_one, 0)

    def first(i, carry):
        at = pl.ds(pl.multiple_of(i * GROUP, GROUP), GROUP)
        acc = jnp.zeros((GROUP, 128), F32)
        for j in range(0, hidden, 128):
            h = h_ref[at, j:j + 128] + part_ref[at, j:j + 128].astype(F32)
            h_ref[at, j:j + 128] = h
            acc += h * h
        r_ref[at, :] = acc
        return carry

    lax.fori_loop(0, span // GROUP, first, 0)
    r = lax.rsqrt(jnp.sum(r_ref[...], axis=1, keepdims=True) * (1.0 / hidden) + RMS_EPS)
    r_ref[...] = jnp.broadcast_to(r, (span, 128))

    def second(i, carry):
        at = pl.ds(pl.multiple_of(i * GROUP, GROUP), GROUP)
        r = r_ref[at, :]
        for j in range(0, hidden, 128):
            xh = (h_ref[at, j:j + 128] * r).astype(BF16).astype(F32)
            y_ref[at, j:j + 128] = (xh * g_ref[:, j:j + 128]).astype(BF16)
        return carry

    lax.fori_loop(0, span // GROUP, second, 0)
    pltpu.make_async_copy(stage.at[pl.ds(0, heads)], de_ref.at[pl.ds(0, heads)], sems.at[1]).wait()


def dense_step(token_ids, table_block, norm_gain, grad_block):
    rows_block, hidden = table_block.shape
    span = grad_block.shape[1]
    tp = lax.axis_index('tp')
    local_ids = token_ids[0] - tp * rows_block
    owned = (local_ids >= 0) & (local_ids < rows_block)
    looked_up = jnp.take(table_block, jnp.where(owned, local_ids, 0), axis=0)
    partial_rows = jnp.where(owned[:, None], looked_up, jnp.zeros((), BF16))
    embedded = lax.dynamic_slice(partial_rows, (tp * span, 0), (span, hidden))
    for flip in (1, 2, 3):
        block = lax.dynamic_slice(partial_rows, ((tp ^ flip) * span, 0), (span, hidden))
        embedded += lax.ppermute(block, 'tp', [(i, i ^ flip) for i in range(4)])
    h = embedded.astype(F32)
    r = lax.rsqrt(jnp.mean(h * h, axis=-1, keepdims=True) + RMS_EPS)
    xh = h * r
    y = xh.astype(BF16) * norm_gain
    dy = grad_block[0].astype(F32)
    dg = jnp.sum(dy * xh, axis=0)
    u = dy * norm_gain.astype(F32)
    dx = (r * (u - xh * jnp.mean(u * xh, axis=-1, keepdims=True))).astype(BF16)
    pair = dg + lax.ppermute(dg, 'tp', SIBLING)
    dg = pair + lax.ppermute(pair, 'tp', ACROSS)
    dx_all = jnp.zeros((4 * span, hidden), F32)
    for flip in (0, 1, 2, 3):
        block = dx if flip == 0 else lax.ppermute(dx, 'tp', [(i, i ^ flip) for i in range(4)])
        dx_all = lax.dynamic_update_slice(dx_all, block.astype(F32), ((tp ^ flip) * span, 0))
    segments = jnp.where(owned, local_ids, rows_block)
    de = jax.ops.segment_sum(dx_all, segments, num_segments=rows_block)
    return y, de, dg


def device_step(token_ids, table_block, norm_gain, grad_block):
    rows, hidden = table_block.shape
    span = grad_block.shape[1]
    dy = grad_block[0]
    slabs = rows // SLAB
    de_shape = jax.ShapeDtypeStruct((slabs, SLAB, hidden), F32)
    zeros = pltpu.VMEM((FILL_STEP, SLAB, hidden), F32)

    packed = pl.pallas_call(
        functools.partial(pack_kernel, rows), out_shape=jax.ShapeDtypeStruct((DY_CAP, hidden), BF16),
        in_specs=[VMEM, VMEM], out_specs=VMEM, compiler_params=pltpu.CompilerParams(vmem_limit_bytes=16 << 20),
        cost_estimate=cost(2, 2 << 20), name='pack')(token_ids, dy)
    dy_got = lax.ppermute(packed, 'tp', ACROSS)
    dy_held, packed = lax.optimization_barrier((dy, packed))
    dy_sib = lax.ppermute(dy_held, 'tp', SIBLING)
    idx, lst, over, rows_u, rows_x, sums, dg8, de = pl.pallas_call(
        functools.partial(main_kernel, rows),
        out_shape=(jax.ShapeDtypeStruct((8, span), jnp.int32), jax.ShapeDtypeStruct((8, 256), jnp.int32),
                   jax.ShapeDtypeStruct((8, 128), F32), jax.ShapeDtypeStruct((U_CAP, hidden), BF16),
                   jax.ShapeDtypeStruct((X_CAP, hidden), BF16), jax.ShapeDtypeStruct((U_CAP, hidden), F32),
                   jax.ShapeDtypeStruct((8, hidden), F32), de_shape),
        in_specs=[VMEM, VMEM, ANY, VMEM], out_specs=(VMEM,) * 7 + (ANY,),
        scratch_shapes=[pltpu.VMEM((8, span), F32), pltpu.VMEM((8, 4 * span), F32), pltpu.SMEM((8, 256), jnp.int32),
                        pltpu.VMEM((U_CAP, SLAB, hidden), BF16), pltpu.VMEM((span, hidden), F32),
                        pltpu.VMEM((span, 128), F32), pltpu.VMEM((span, 128), F32), pltpu.VMEM((span, hidden), BF16),
                        pltpu.VMEM((1, hidden), F32), zeros, pltpu.SemaphoreType.DMA((3,))],
        compiler_params=pltpu.CompilerParams(vmem_limit_bytes=36 << 20),
        cost_estimate=cost(12, 40 << 20), name='main')(
            token_ids, dy, table_block.reshape(slabs, SLAB, hidden), norm_gain)
    u_got = lax.ppermute(rows_x, 'tp', ACROSS)
    u_sib = lax.ppermute(rows_u, 'tp', SIBLING)

    def zero(de, lo, hi):
        return pl.pallas_call(
            functools.partial(zero_kernel, lo, hi), out_shape=de_shape, in_specs=[ANY], out_specs=ANY,
            input_output_aliases={0: 0}, scratch_shapes=[zeros, pltpu.SemaphoreType.DMA],
            compiler_params=pltpu.CompilerParams(vmem_limit_bytes=8 << 20),
            cost_estimate=cost(8, 20 << 20), name='zero')(de)

    de = zero(de, FILLS[2], FILLS[3])
    dy_got, over, de = lax.optimization_barrier((dy_got, over, de))
    dy_fwd = lax.ppermute(dy_got, 'tp', SIBLING)
    over = jnp.maximum(over, lax.ppermute(over, 'dp', [(i, i ^ 1) for i in range(4)]))
    sums, dg, part, de = pl.pallas_call(
        token_kernel,
        out_shape=(jax.ShapeDtypeStruct((U_CAP, hidden), F32), jax.ShapeDtypeStruct((1, hidden), F32),
                   jax.ShapeDtypeStruct((span, hidden), BF16), de_shape),
        in_specs=[VMEM] * 9 + [ANY], out_specs=(VMEM, VMEM, VMEM, ANY), input_output_aliases={9: 3},
        scratch_shapes=[pltpu.VMEM((span, hidden), F32), pltpu.VMEM((span, 128), F32), pltpu.VMEM((span, 128), F32),
                        pltpu.VMEM((span, hidden), BF16), pltpu.VMEM((8, hidden), F32), pltpu.VMEM((1, hidden), F32),
                        zeros, pltpu.SemaphoreType.DMA],
        compiler_params=pltpu.CompilerParams(vmem_limit_bytes=32 << 20),
        cost_estimate=cost(8, 16 << 20), name='tokens')(
            idx, rows_u, u_sib, dy_sib, dy_got, dy_fwd, sums, dg8, norm_gain, de)
    dgs = [dg]
    for f in (1, 2, 3):
        dgs.append(lax.ppermute(dg, 'tp', [(i, i ^ f) for i in range(4)]))
    u_got, part, over = lax.optimization_barrier((u_got, part, over))
    u_fwd = lax.ppermute(u_got, 'tp', SIBLING)
    over = jnp.maximum(over, lax.ppermute(over, 'dp', [(i, i ^ 2) for i in range(4)]))
    if FILLS[5] > FILLS[4]:
        de = zero(de, FILLS[4], FILLS[5])
    y, dg, over, de = pl.pallas_call(
        final_kernel,
        out_shape=(jax.ShapeDtypeStruct((span, hidden), BF16), jax.ShapeDtypeStruct((1, hidden), F32),
                   jax.ShapeDtypeStruct((1, 1), jnp.int32), de_shape),
        in_specs=[VMEM] * 12 + [ANY], out_specs=(VMEM, VMEM, VMEM, ANY), input_output_aliases={12: 3},
        scratch_shapes=[pltpu.SMEM((8, 256), jnp.int32), pltpu.VMEM((U_CAP, SLAB, hidden), F32), pltpu.VMEM((span, hidden), F32),
                        pltpu.VMEM((span, 128), F32), pltpu.VMEM((1, hidden), F32), zeros, pltpu.SemaphoreType.DMA((3,))],
        compiler_params=pltpu.CompilerParams(vmem_limit_bytes=32 << 20),
        cost_estimate=cost(5, 8 << 20), name='final')(lst, over, idx, sums, part, u_got, u_fwd, norm_gain, *dgs, de)

    def keep(y, de, dg):
        return y, de, dg

    def redo(y, de, dg):
        y, de, dg = dense_step(token_ids, table_block, norm_gain, grad_block)
        return y, de.reshape(slabs, SLAB, hidden), dg.reshape(1, hidden)

    y, de, dg = lax.cond(over.reshape(()) > 0, redo, keep, y, de, dg)
    return y[None], de.reshape(rows, hidden), dg.reshape(hidden)


def solution(mesh):
    return jax.shard_map(device_step, mesh=mesh, in_specs=(P('dp', None), P('tp', None), P(None), P('dp', 'tp', None)), out_specs=(P('dp', 'tp', None), P(('dp', 'tp'), None), P('dp')), check_vma=False)
```

time: 86.6 us -> 48.3 us (0.56)
  Pallas kernels: 54.6 us -> 33.3 us
  waiting for transfers between devices: 15.3 us -> 3.37 us
  local copies, waits for them, and re-layouts: 4.53 us -> 0.02 us
    pallas_call x6 -> x5, Pallas kernels: 52 us -> 31.5 us  [the longest x1 14.7 us: device_step(): pl.pallas_call(functools.partial(main_kernel, rows), out_shape=(jax.Shape...]
    ppermute x1, waiting for transfers between devices: 6.43 us -> 0.01 us  [device_step(): dy_got = lax.ppermute(packed, 'tp', ACROSS)]
    ppermute x5, waiting for transfers between devices: 7.07 us -> 1.61 us  [the longest x1 1.6 us: device_step(): u_got = lax.ppermute(rows_x, 'tp', ACROSS)]
    unnamed x20 -> x6, local copies, waits for them, and re-layouts: 2.39 us -> 0.02 us
    slice x2 -> x0, local copies, waits for them, and re-layouts: 1.54 us -> none  [the longest x1 1.02 us: device_step(): u_got = lax.ppermute(rows_u[:X_CAP], 'tp', ACROSS)]
  transfers between devices with their start and end apart: 11 -> 11, of which waited for: 3 -> 2; matrix products, arithmetic and copies ran while one was open for 3% -> 0% of each run, Pallas kernels for 56% -> 54%
where the time goes in v2:
time: 48.3 us; the launch traced here: 48 us
  Pallas kernels  33.3 us (69%)
  starting transfers between devices  9.61 us (20%)
  waiting for transfers between devices  3.37 us (7%)
  between operations  1.52 us (3%)
    pallas_call x1, Pallas kernels, device_step(): pl.pallas_call(functools.partial(main_kernel, rows), out_shape=(jax.Shape...  14.7 us
    pallas_call x1, Pallas kernels, device_step(): pl.pallas_call(token_kernel, out_shape=(jax.ShapeDtypeStruct((U_CAP, hidd...  6.03 us
    pallas_call x1, Pallas kernels, device_step(): pl.pallas_call(final_kernel, out_shape=(jax.ShapeDtypeStruct((span, hidde...  5.51 us
    pallas_call x2, Pallas kernels, zero(): pl.pallas_call(functools.partial(zero_kernel, lo, hi), out_shape=de_shape...  5.32 us
    ppermute x1, starting transfers between devices, device_step(): dy_got = lax.ppermute(packed, 'tp', ACROSS)  3.23 us
    ppermute x3, starting transfers between devices, device_step(): dgs.append(lax.ppermute(dg, 'tp', [(i, i ^ f) for i in range(4)]))  2.14 us
    ppermute x1, starting transfers between devices, device_step(): lax.ppermute(over, 'dp', [(i, i ^ 1) for i in range(4)])  1.86 us
    ppermute x1, waiting for transfers between devices, device_step(): lax.ppermute(over, 'dp', [(i, i ^ 1) for i in range(4)])  1.75 us
  transfers between devices with their start and end apart: 11, of which 2 were waited for; matrix products, arithmetic and copies ran while one was open for 0% of the time, Pallas kernels for 54%

profile of v2, /device:TPU:0, one launch (start us, length us, event | category | flops | bytes accessed | tf_op | source)
XLA Modules:
  0.0 48.0 jit_solution(6790893194077652549)
XLA Ops:
  0.6 1.7 %pack.1 = bf16[176,2048]{1,0:T(8,128)(2,1)S(1)} custom-call(s32[1,1024]{1,0:T(1,128)} %ids_ref.3, bf16[256,2048]{1,0:T(8,128)(2,1)} %bitcast.22), custom_call_target="tpu_custom_call" | custom-call | flops 4000000 | bytes 2097152 | tf_op jit(solution)/shard_map/pack/pallas_call | solution.py:417
  2.4 3.2 %collective-permute-start.11 = (bf16[176,2048]{1,0:T(8,128)(2,1)S(1)}, bf16[176,2048]{1,0:T(8,128)(2,1)S(1)}, u32[]{:S(2)}, u32[]{:S(2)}) collective-permute-start(bf16[176,2048]{1,0:T(8,128)(2,1)S(1)} %pack.1), channel_id=1, source_target_pairs={{0,2},{1,3},{2,0},{3,1},{4,6},{5,7},{6,4},{7,5},{8,10},{9,11},{10,... | collective-permute-start | bytes 2162696 | tf_op jit(solution)/shard_map/ppermute | solution.py:421
  5.6 0.0 collective-permute-start.10
  5.6 14.7 %main.1 = (s32[8,256]{1,0:T(8,128)S(1)}, s32[8,256]{1,0:T(8,128)S(1)}, f32[8,128]{1,0:T(8,128)S(1)}, bf16[144,2048]{1,0:T(8,128)(2,1)S(1)}, bf16[96,2048]{1,0:T(...) custom-call(s32[1,1024]{1,0:T(1,128)} %ids_ref.3, ...), custom_call_target="tpu_custom_call" | custom-call | flops 24000000 | bytes 41943040 | tf_op jit(solution)/shard_map/main/pallas_call | solution.py:424
  20.3 0.0 copy-start.4
  20.3 2.9 %zero.2.de_in = f32[1000,8,2048]{2,1,0:T(8,128)} custom-call(f32[1000,8,2048]{2,1,0:T(8,128)} %get-tuple-element.59.de_in), custom_call_target="tpu_custom_call", output_to_operand_aliasing={{}: (0, {})} | custom-call | flops 16000000 | bytes 20971520 | tf_op jit(solution)/shard_map/zero/pallas_call | solution.py:442
  23.2 0.0 collective-permute-done.11.got_ref
  23.2 0.5 %collective-permute-start.12 = (bf16[176,2048]{1,0:T(8,128)(2,1)S(1)}, bf16[176,2048]{1,0:T(8,128)(2,1)S(1)}, u32[]{:S(2)}, u32[]{:S(2)}) collective-permute-start(bf16[176,2048]{1,0:T(8,128)(2,1)S(1)} %collective-permute-done.11.got_ref), channel_id=1, source_target_pairs={{0,1},{1,0},{2,3},{3,2},{4,5},{5,4},{6,7},{7,6},{8,9},{9,8},{10,11... | collective-permute-start | bytes 2162696 | tf_op jit(solution)/shard_map/ppermute | solution.py:450
  23.7 0.0 collective-permute-start.9
  23.8 0.2 collective-permute-start.8
  24.0 1.9 %collective-permute-start.13 = (f32[8,128]{1,0:T(8,128)S(1)}, f32[8,128]{1,0:T(8,128)S(1)}, u32[]{:S(2)}, u32[]{:S(2)}) collective-permute-start(f32[8,128]{1,0:T(8,128)S(1)} %get-tuple-element.65), channel_id=1, source_target_pairs={{0,4},{4,0},{8,12},{12,8},{1,5},{5,1},{9,13},{13,9},{2,6},{6,2},{1... | collective-permute-start | bytes 12296 | tf_op jit(solution)/shard_map/ppermute | solution.py:451
  25.9 1.8 %collective-permute-done.13 = f32[8,128]{1,0:T(8,128)S(1)} collective-permute-done((f32[8,128]{1,0:T(8,128)S(1)}, f32[8,128]{1,0:T(8,128)S(1)}, u32[]{:S(2)}, u32[]{:S(2)}) %collective-permute-start.13) | collective-permute-done | bytes 4128 | tf_op jit(solution)/shard_map/ppermute | solution.py:451
  27.6 0.0 collective-permute-done.10.sib_ref
  27.6 6.0 %tokens.1 = (f32[144,2048]{1,0:T(8,128)S(1)}, f32[1,2048]{1,0:T(1,128)S(1)}, bf16[256,2048]{1,0:T(8,128)(2,1)S(1)}, f32[1000,8,2048]{2,1,0:T(8,128)}) custom-call(s32[8,256]{1,0:T(8,128)S(1)} %get-tuple-element.55.idx_ref, bf16[144,2048]{1,0:T(8,128)(2,1)S(1)} %get-tuple-element.56.u_ref, ...), custom_call_target="tpu_custom_call", output_to_operand_aliasing={{3}: (9, {})} | custom-call | flops 16000000 | bytes 16777216 | tf_op jit(solution)/shard_map/tokens/pallas_call | solution.py:452
  33.7 1.6 %collective-permute-done.8.got_ref = bf16[96,2048]{1,0:T(8,128)(2,1)S(1)} collective-permute-done((bf16[96,2048]{1,0:T(8,128)(2,1)S(1)}, bf16[96,2048]{1,0:T(8,128)(2,1)S(1)}, u32[]{:S(2)}, u32[]{:S(2)}) %collective-permute-start.8) | collective-permute-done | bytes 393248 | tf_op jit(solution)/shard_map/ppermute | solution.py:438
  35.3 0.0 collective-permute-start.15
  35.3 0.4 collective-permute-start.18
  35.7 1.7 %collective-permute-start.17 = (f32[1,2048]{1,0:T(1,128)S(1)}, f32[1,2048]{1,0:T(1,128)S(1)}, u32[]{:S(2)}, u32[]{:S(2)}) collective-permute-start(f32[1,2048]{1,0:T(1,128)S(1)} %get-tuple-element.70.g0), channel_id=1, source_target_pairs={{0,2},{1,3},{2,0},{3,1},{4,6},{5,7},{6,4},{7,5},{8,10},{9,11},{10,... | collective-permute-start | bytes 24584 | tf_op jit(solution)/shard_map/ppermute | solution.py:465
  37.4 1.6 %collective-permute-start.14 = (f32[8,128]{1,0:T(8,128)S(1)}, f32[8,128]{1,0:T(8,128)S(1)}, u32[]{:S(2)}, u32[]{:S(2)}) collective-permute-start(f32[8,128]{1,0:T(8,128)S(1)} %max.6), channel_id=1, source_target_pairs={{0,8},{4,12},{8,0},{12,4},{1,9},{5,13},{9,1},{13,5},{2,10},{6,14},... | collective-permute-start | bytes 12296 | tf_op jit(solution)/shard_map/ppermute | solution.py:468
  39.0 2.4 %zero.3.de_in = f32[1000,8,2048]{2,1,0:T(8,128)} custom-call(f32[1000,8,2048]{2,1,0:T(8,128)} %get-tuple-element.71.de_in), custom_call_target="tpu_custom_call", output_to_operand_aliasing={{}: (0, {})} | custom-call | flops 16000000 | bytes 20971520 | tf_op jit(solution)/shard_map/zero/pallas_call | solution.py:442
  41.5 0.0 copy-start
  41.5 0.0 copy-start.5
  41.5 5.5 %final.1 = (bf16[256,2048]{1,0:T(8,128)(2,1)}, f32[1,2048]{1,0:T(1,128)}, s32[1,1]{1,0:T(1,128)}, f32[1000,8,2048]{2,1,0:T(8,128)}) custom-call(s32[8,256]{1,0:T(8,128)S(1)} %get-tuple-element.53.tab_ref, f32[8,128]{1,0:T(8,128)S(1)} %max.7.flag_ref, s32[8,256]{1,0:T(8,128)S(1)} %get-tuple-element.55.idx_ref, ...), custom_call_target="tpu_custom_call", output_to_operand_aliasing={{3}: (12, {})} | custom-call | flops 10000000 | bytes 8388608 | tf_op jit(solution)/shard_map/final/pallas_call | solution.py:471
  47.6 0.2 conditional.1
  (13 shorter events, 0.0 us)
Async XLA Ops:
  2.4 20.8 %collective-permute-start.11 = (bf16[176,2048]{1,0:T(8,128)(2,1)S(1)}, bf16[176,2048]{1,0:T(8,128)(2,1)S(1)}, u32[]{:S(2)}, u32[]{:S(2)}) collective-permute-start(bf16[176,2048]{1,0:T(8,128)(2,1)S(1)} %pack.1), channel_id=1, source_target_pairs={{0,2},{1,3},{2,0},{3,1},{4,6},{5,7},{6,4},{7,5},{8,10},{9,11},{10,... | collective-permute-start | bytes 2162696 | tf_op jit(solution)/shard_map/ppermute | solution.py:421
  5.6 22.0 %collective-permute-start.10 = (bf16[256,2048]{1,0:T(8,128)(2,1)}, bf16[256,2048]{1,0:T(8,128)(2,1)S(1)}, u32[]{:S(2)}, u32[]{:S(2)}) collective-permute-start(bf16[256,2048]{1,0:T(8,128)(2,1)} %bitcast.23), channel_id=1, source_target_pairs={{0,1},{1,0},{2,3},{3,2},{4,5},{5,4},{6,7},{7,6},{8,9},{9,8},{10,11... | collective-permute-start | bytes 3145736 | tf_op jit(solution)/shard_map/ppermute | solution.py:423
  20.3 7.3 %copy-start.4 = (bf16[2048]{0:T(1024)(128)(2,1)S(1)}, bf16[2048]{0:T(1024)(128)(2,1)}, u32[]{:S(2)}) copy-start(bf16[2048]{0:T(1024)(128)(2,1)} %gain_ref.5) | copy-start | bytes 12292
  23.2 4.4 %collective-permute-start.12 = (bf16[176,2048]{1,0:T(8,128)(2,1)S(1)}, bf16[176,2048]{1,0:T(8,128)(2,1)S(1)}, u32[]{:S(2)}, u32[]{:S(2)}) collective-permute-start(bf16[176,2048]{1,0:T(8,128)(2,1)S(1)} %collective-permute-done.11.got_ref), channel_id=1, source_target_pairs={{0,1},{1,0},{2,3},{3,2},{4,5},{5,4},{6,7},{7,6},{8,9},{9,8},{10,11... | collective-permute-start | bytes 2162696 | tf_op jit(solution)/shard_map/ppermute | solution.py:450
  23.7 3.9 %collective-permute-start.9 = (bf16[144,2048]{1,0:T(8,128)(2,1)S(1)}, bf16[144,2048]{1,0:T(8,128)(2,1)S(1)}, u32[]{:S(2)}, u32[]{:S(2)}) collective-permute-start(bf16[144,2048]{1,0:T(8,128)(2,1)S(1)} %get-tuple-element.56.u_ref), channel_id=1, source_target_pairs={{0,1},{1,0},{2,3},{3,2},{4,5},{5,4},{6,7},{7,6},{8,9},{9,8},{10,11... | collective-permute-start | bytes 1769480 | tf_op jit(solution)/shard_map/ppermute | solution.py:439
  23.8 11.5 %collective-permute-start.8 = (bf16[96,2048]{1,0:T(8,128)(2,1)S(1)}, bf16[96,2048]{1,0:T(8,128)(2,1)S(1)}, u32[]{:S(2)}, u32[]{:S(2)}) collective-permute-start(bf16[96,2048]{1,0:T(8,128)(2,1)S(1)} %get-tuple-element.54), channel_id=1, source_target_pairs={{0,2},{1,3},{2,0},{3,1},{4,6},{5,7},{6,4},{7,5},{8,10},{9,11},{10,... | collective-permute-start | bytes 1179656 | tf_op jit(solution)/shard_map/ppermute | solution.py:438
  24.0 3.6 %collective-permute-start.13 = (f32[8,128]{1,0:T(8,128)S(1)}, f32[8,128]{1,0:T(8,128)S(1)}, u32[]{:S(2)}, u32[]{:S(2)}) collective-permute-start(f32[8,128]{1,0:T(8,128)S(1)} %get-tuple-element.65), channel_id=1, source_target_pairs={{0,4},{4,0},{8,12},{12,8},{1,5},{5,1},{9,13},{13,9},{2,6},{6,2},{1... | collective-permute-start | bytes 12296 | tf_op jit(solution)/shard_map/ppermute | solution.py:451
  35.3 6.2 %collective-permute-start.15 = (bf16[96,2048]{1,0:T(8,128)(2,1)S(1)}, bf16[96,2048]{1,0:T(8,128)(2,1)S(1)}, u32[]{:S(2)}, u32[]{:S(2)}) collective-permute-start(bf16[96,2048]{1,0:T(8,128)(2,1)S(1)} %collective-permute-done.8.got_ref), channel_id=1, source_target_pairs={{0,1},{1,0},{2,3},{3,2},{4,5},{5,4},{6,7},{7,6},{8,9},{9,8},{10,11... | collective-permute-start | bytes 1179656 | tf_op jit(solution)/shard_map/ppermute | solution.py:467
  35.3 6.2 %collective-permute-start.18 = (f32[1,2048]{1,0:T(1,128)S(1)}, f32[1,2048]{1,0:T(1,128)S(1)}, u32[]{:S(2)}, u32[]{:S(2)}) collective-permute-start(f32[1,2048]{1,0:T(1,128)S(1)} %get-tuple-element.70.g0), channel_id=1, source_target_pairs={{0,3},{1,2},{2,1},{3,0},{4,7},{5,6},{6,5},{7,4},{8,11},{9,10},{10,... | collective-permute-start | bytes 24584 | tf_op jit(solution)/shard_map/ppermute | solution.py:465
  35.7 5.8 %collective-permute-start.17 = (f32[1,2048]{1,0:T(1,128)S(1)}, f32[1,2048]{1,0:T(1,128)S(1)}, u32[]{:S(2)}, u32[]{:S(2)}) collective-permute-start(f32[1,2048]{1,0:T(1,128)S(1)} %get-tuple-element.70.g0), channel_id=1, source_target_pairs={{0,2},{1,3},{2,0},{3,1},{4,6},{5,7},{6,4},{7,5},{8,10},{9,11},{10,... | collective-permute-start | bytes 24584 | tf_op jit(solution)/shard_map/ppermute | solution.py:465
  37.4 4.1 %collective-permute-start.16 = (f32[1,2048]{1,0:T(1,128)S(1)}, f32[1,2048]{1,0:T(1,128)S(1)}, u32[]{:S(2)}, u32[]{:S(2)}) collective-permute-start(f32[1,2048]{1,0:T(1,128)S(1)} %get-tuple-element.70.g0), channel_id=1, source_target_pairs={{0,1},{1,0},{2,3},{3,2},{4,5},{5,4},{6,7},{7,6},{8,9},{9,8},{10,11... | collective-permute-start | bytes 24584 | tf_op jit(solution)/shard_map/ppermute | solution.py:465
  37.4 4.0 %collective-permute-start.14 = (f32[8,128]{1,0:T(8,128)S(1)}, f32[8,128]{1,0:T(8,128)S(1)}, u32[]{:S(2)}, u32[]{:S(2)}) collective-permute-start(f32[8,128]{1,0:T(8,128)S(1)} %max.6), channel_id=1, source_target_pairs={{0,8},{4,12},{8,0},{12,4},{1,9},{5,13},{9,1},{13,5},{2,10},{6,14},... | collective-permute-start | bytes 12296 | tf_op jit(solution)/shard_map/ppermute | solution.py:468
  41.5 6.1 %copy-start = (bf16[1,256,2048]{2,1,0:T(8,128)(2,1)S(1)}, bf16[1,256,2048]{2,1,0:T(8,128)(2,1)}, u32[]{:S(2)}) copy-start(bf16[1,256,2048]{2,1,0:T(8,128)(2,1)} %param.9) | copy-start | bytes 3145732
  41.5 6.1 %copy-start.5 = (s32[1,1024]{1,0:T(1,128)S(1)}, s32[1,1024]{1,0:T(1,128)}, u32[]{:S(2)}) copy-start(s32[1,1024]{1,0:T(1,128)} %ids_ref.3) | copy-start | bytes 12292
